TPU v7x, 8 devices: a whole 2x2x1 slice. The times are simulated.
8 devices in a mesh: dp: 2 (over z, y), tp: 4 (over x, core).
Axes of the slice: x: 2, y: 2, z: 1, core: 2. Of those that a mesh axis runs over, the one named last changes fastest.
Arguments:
- tok_hidden: bfloat16 [256, 2048], P('dp'), parts along dimension 0
- seq_lens: int32 [256], P('dp'), parts along dimension 0
- k_cache: bfloat16 [256, 512, 4, 128], P('dp', None, 'tp'), parts along dimension 0
- v_cache: bfloat16 [256, 512, 4, 128], P('dp', None, 'tp'), parts along dimension 0
- next_tok: int32 [256], P('dp'), parts along dimension 0
- g_attn: bfloat16 [2048], replicated
- w_q: bfloat16 [2048, 2048], P(None, 'tp')
- b_q: bfloat16 [2048], P('tp')
- w_k: bfloat16 [2048, 512], P(None, 'tp')
- b_k: bfloat16 [512], P('tp')
- w_v: bfloat16 [2048, 512], P(None, 'tp')
- b_v: bfloat16 [512], P('tp')
- w_o: bfloat16 [2048, 2048], P('tp')
- g_mlp: bfloat16 [2048], replicated
- w_gate: bfloat16 [2048, 11008], P(None, 'tp')
- w_up: bfloat16 [2048, 11008], P(None, 'tp')
- w_down: bfloat16 [11008, 2048], P('tp')
- g_final: bfloat16 [2048], replicated
- w_head: bfloat16 [151936, 2048], P('tp')
Outputs:
- output 1: bfloat16 [256, 2048], P('dp'), parts along dimension 0
- output 2: bfloat16 [256, 512, 4, 128], P('dp', None, 'tp'), parts along dimension 0
- output 3: bfloat16 [256, 512, 4, 128], P('dp', None, 'tp'), parts along dimension 0
- output 4: float32 [256], P('dp'), parts along dimension 0
- output 5: float32 [256], P('dp'), parts along dimension 0
There are 2 independent parts. A program takes and returns all parts, laid end to end along the dimension named above; an argument that names none is the same for every part.
All inputs are finite; a program needn't handle non-finite values.
Results may differ from a plain program's by a relative error of at most 0.0126882.
Values are sent between devices in bfloat16 or wider.
A program may use at most 1 GiB of HBM per device.

v0:
```python
import jax
import jax.numpy as jnp
from jax import lax
from jax.sharding import PartitionSpec as P

THETA = 1000000.0
EPS = 1e-6


def rms_norm(values, gain_vec):
    vals_f32 = values.astype(jnp.float32)
    inv_rms = lax.rsqrt(jnp.mean(vals_f32 * vals_f32, axis=-1, keepdims=True) + EPS)
    return (vals_f32 * inv_rms * gain_vec.astype(jnp.float32)).astype(jnp.bfloat16)


def rotary(values, positions):
    half_dim = values.shape[-1] // 2
    inv_freq = jnp.power(THETA, jnp.arange(half_dim, dtype=jnp.float32) * (-2.0 / values.shape[-1]))
    angles = positions.astype(jnp.float32)[:, None] * inv_freq[None, :]
    cos_part = jnp.cos(angles)[:, None, :]
    sin_part = jnp.sin(angles)[:, None, :]
    first_half = values[..., :half_dim]
    second_half = values[..., half_dim:]
    return jnp.concatenate([first_half * cos_part - second_half * sin_part, second_half * cos_part + first_half * sin_part], axis=-1)


def attention_block(tok_hidden, seq_lens, k_cache, v_cache, g_attn, w_q, b_q, w_k, b_k, w_v, b_v):
    num_rows = tok_hidden.shape[0]
    cache_len = k_cache.shape[1]
    slot_count = k_cache.shape[2]
    head_dim = k_cache.shape[3]
    head_count = w_q.shape[1] // head_dim
    group_size = head_count // slot_count
    normed = rms_norm(tok_hidden, g_attn)
    q_proj = jnp.dot(normed, w_q, preferred_element_type=jnp.float32) + b_q.astype(jnp.float32)
    k_proj = jnp.dot(normed, w_k, preferred_element_type=jnp.float32) + b_k.astype(jnp.float32)
    v_proj = jnp.dot(normed, w_v, preferred_element_type=jnp.float32) + b_v.astype(jnp.float32)
    q_rot = rotary(q_proj.reshape(num_rows, head_count, head_dim), seq_lens).astype(jnp.bfloat16)
    k_new = rotary(k_proj.reshape(num_rows, slot_count, head_dim), seq_lens).astype(jnp.bfloat16)
    v_new = v_proj.reshape(num_rows, slot_count, head_dim).astype(jnp.bfloat16)
    slot_ids = lax.broadcasted_iota(jnp.int32, (1, cache_len, 1, 1), 1)
    write_mask = slot_ids == seq_lens[:, None, None, None]
    k_all = jnp.where(write_mask, k_new[:, None], k_cache)
    v_all = jnp.where(write_mask, v_new[:, None], v_cache)
    q_grp = q_rot.reshape(num_rows, slot_count, group_size, head_dim)
    scores = jnp.einsum('bkgd,blkd->bkgl', q_grp, k_all, preferred_element_type=jnp.float32) * (head_dim ** -0.5)
    score_ids = lax.broadcasted_iota(jnp.int32, (1, 1, 1, cache_len), 3)
    scores = jnp.where(score_ids <= seq_lens[:, None, None, None], scores, -jnp.inf)
    row_max = jnp.max(scores, axis=-1, keepdims=True)
    exp_scores = jnp.exp(scores - row_max)
    attn_probs = (exp_scores / jnp.sum(exp_scores, axis=-1, keepdims=True)).astype(jnp.bfloat16)
    attn_vals = jnp.einsum('bkgl,blkd->bkgd', attn_probs, v_all, preferred_element_type=jnp.float32)
    attn_out = attn_vals.astype(jnp.bfloat16).reshape(num_rows, head_count * head_dim)
    return attn_out, k_all, v_all


def local_step(tok_hidden, seq_lens, k_cache, v_cache, next_tok, g_attn, w_q, b_q, w_k, b_k, w_v, b_v, w_o, g_mlp, w_gate, w_up, w_down, g_final, w_head):
    attn_out, k_all, v_all = attention_block(tok_hidden, seq_lens, k_cache, v_cache, g_attn, w_q, b_q, w_k, b_k, w_v, b_v)
    attn_part = jnp.dot(attn_out, w_o, preferred_element_type=jnp.float32).astype(jnp.bfloat16)
    attn_sum = lax.psum(attn_part, 'tp')
    residual = (tok_hidden.astype(jnp.float32) + attn_sum.astype(jnp.float32)).astype(jnp.bfloat16)
    mlp_in = rms_norm(residual, g_mlp)
    gate_proj = jnp.dot(mlp_in, w_gate, preferred_element_type=jnp.float32)
    up_proj = jnp.dot(mlp_in, w_up, preferred_element_type=jnp.float32)
    hidden = (jax.nn.silu(gate_proj) * up_proj).astype(jnp.bfloat16)
    down_part = jnp.dot(hidden, w_down, preferred_element_type=jnp.float32).astype(jnp.bfloat16)
    down_sum = lax.psum(down_part, 'tp')
    y_out = (residual.astype(jnp.float32) + down_sum.astype(jnp.float32)).astype(jnp.bfloat16)
    final_norm = rms_norm(y_out, g_final)
    logits = lax.dot_general(final_norm, w_head, (((1,), (1,)), ((), ())), preferred_element_type=jnp.float32)
    vocab_loc = w_head.shape[0]
    vocab_ids = lax.broadcasted_iota(jnp.int32, (1, vocab_loc), 1)
    local_tok = next_tok - lax.axis_index('tp') * vocab_loc
    local_max = jnp.max(logits, axis=1)
    local_sum = jnp.sum(jnp.exp(logits - local_max[:, None]), axis=1)
    local_target = jnp.sum(jnp.where(vocab_ids == local_tok[:, None], logits, 0.0), axis=1)
    all_stats = lax.all_gather(jnp.stack([local_max, local_sum, local_target]), 'tp')
    glob_max = jnp.max(all_stats[:, 0], axis=0)
    exp_total = jnp.sum(all_stats[:, 1] * jnp.exp(all_stats[:, 0] - glob_max[None, :]), axis=0)
    norm_lse = glob_max + jnp.log(exp_total)
    tok_logp = jnp.sum(all_stats[:, 2], axis=0) - norm_lse
    return y_out, k_all, v_all, tok_logp, norm_lse


def solution(mesh):
    row_spec = P('dp', None)
    vec_spec = P('dp')
    cache_spec = P('dp', None, 'tp', None)
    col_spec = P(None, 'tp')
    part_spec = P('tp')
    whole_spec = P(None)
    in_specs = (row_spec, vec_spec, cache_spec, cache_spec, vec_spec, whole_spec, col_spec, part_spec, col_spec, part_spec, col_spec, part_spec, P('tp', None), whole_spec, col_spec, col_spec, P('tp', None), whole_spec, P('tp', None))
    out_specs = (row_spec, cache_spec, cache_spec, vec_spec, vec_spec)
    return jax.shard_map(local_step, mesh=mesh, in_specs=in_specs, out_specs=out_specs, check_vma=False)
```

profile of v0, /device:TPU:0, one launch (start us, length us, event | category | flops | bytes accessed | tf_op | source)
XLA Modules:
  0.0 235.9 jit_solution(11175741312991618947)
XLA Ops:
  7.2 0.0 all-reduce.3.cloned.1.call-start
  7.2 0.8 convert_element_type.89
  8.0 0.8 iota_compare_fusion.2
  8.8 0.7 convert_element_type.86
  9.5 1.2 fusion.22
  10.8 0.7 convert_element_type.90
  11.4 0.3 multiply_cosine_fusion
  11.7 1.6 fusion.14
  13.4 0.2 fusion.53
  13.6 0.1 copy.26
  13.7 0.7 convert_element_type.92
  14.4 0.7 convert_element_type.88
  15.0 2.3 convolution_add_fusion
  17.3 0.1 reshape.267
  17.4 1.6 fusion.18
  19.0 0.3 subtract_convert_fusion
  19.3 23.3 %broadcast_select_fusion.1 = (bf16[128,512,1,128]{3,1,2,0:T(8,128)(2,1)}, bf16[128,512,1,128]{3,1,2,0:T(8,128)(2,1)}) fusion(bf16[128,512,1,128]{3,1,2,0:T(8,128)(2,1)} %param.21, pred[128,512]{1,0:T(8,128)(4,1)S(1)} %get-tuple-element.26, bf16[128,128]{1,0:T(8,128)(2,1)S(1)} %copy.26, bf16[128,512,1,128]{3,1,2,0:T(8,128)(2,1)} %param.22, ...), kind=kLoop, calls=%fused_computation.9 | loop fusion | flops 16777216 | bytes 67239936 | tf_op jit(solution)/shard_map/jit(_where)/select_n | solution.py:43
  42.6 10.4 %fusion.62 = (f32[128,4]{1,0:T(8,128)S(1)}, f32[128,4,512]{2,1,0:T(4,128)S(1)}) fusion(bf16[128,512,1,128]{3,1,2,0:T(8,128)(2,1)} %get-tuple-element.19, pred[128,512]{1,0:T(8,128)(4,1)S(1)} %get-tuple-element.25, bf16[128,4,64]{2,1,0:T(4,128)(2,1)S(1)} %get-tuple-element.16, bf16[128,4,64]{2,1,0:T(4,128)(2,1)S(1)} %get-tuple-element.15), kind=kOutput, calls=%fused_computation.86 | convolution fusion | flops 68420096 | bytes 18024448 | tf_op jit(solution)/shard_map/sub | solution.py:50
  53.0 7.1 %fusion.11 = bf16[128,4,128]{2,1,0:T(4,128)(2,1)S(1)} fusion(bf16[128,512,1,128]{3,1,2,0:T(8,128)(2,1)} %get-tuple-element.20, f32[128,4,512]{2,1,0:T(4,128)S(1)} %get-tuple-element.28, f32[128,4]{1,0:T(8,128)S(1)} %get-tuple-element.27), kind=kOutput, calls=%fused_computation.26 | convolution fusion | flops 67698688 | bytes 17958912 | tf_op jit(solution)/shard_map/bkgl,blkd->bkgd/dot_general | solution.py:52
  60.1 1.3 convolution_convert_fusion.1
  61.4 0.2 all-reduce.5.cloned.1.call-start
  61.6 30.5 %all-reduce.3.cloned.1.call-done = bf16[128,2048]{1,0:T(8,128)(2,1)} async-done(((bf16[128,2048]{1,0:T(8,128)(2,1)}), bf16[128,2048]{1,0:T(8,128)(2,1)}) %all-reduce.3.cloned.1.call-update) | async-done | bytes 524304 | tf_op jit(solution)/shard_map/psum | solution.py:60
  92.1 1.5 fusion.26
  93.6 6.0 %fusion.37 = f32[128,2752]{0,1:T(8,128)S(1)} fusion(bf16[2048,2752]{0,1:T(8,128)(2,1)} %param.33, bf16[128,2048]{1,0:T(8,128)(2,1)S(1)} %get-tuple-element.14, f32[2048]{0:T(1024)S(1)} %convert_element_type.99, f32[128]{0:T(128)S(1)} %add_rsqrt_fusion.1), kind=kOutput, calls=%fused_computation.52 | convolution fusion | flops 1443889152 | bytes 13214208 | tf_op jit(solution)/shard_map/dot_general | solution.py:63
  99.7 15.4 %convolution_convert_fusion = bf16[128,2048]{1,0:T(8,128)(2,1)} fusion(bf16[2752,2048]{1,0:T(8,128)(2,1)} %param.35, bf16[2048,2752]{0,1:T(8,128)(2,1)} %param.34, f32[128,2752]{0,1:T(8,128)S(1)} %fusion.37, bf16[128,2048]{1,0:T(8,128)(2,1)S(1)} %get-tuple-element.14, f32[2048]{0:T(1024)S(1)} %convert_element_type.99, f32[128]{0:T(128)S(1)} %add_rsqrt_fusion.1), kind=kOutput, calls=%fused_computation.12 | convolution fusion | flops 2889105408 | bytes 25010688 | tf_op jit(solution)/shard_map/dot_general | solution.py:66
  115.0 0.0 all-reduce.5.cloned.1.call-update
  115.1 27.9 %all-reduce.5.cloned.1.call-done = bf16[128,2048]{1,0:T(8,128)(2,1)} async-done(((bf16[128,2048]{1,0:T(8,128)(2,1)}), bf16[128,2048]{1,0:T(8,128)(2,1)}) %all-reduce.5.cloned.1.call-update) | async-done | bytes 524304 | tf_op jit(solution)/shard_map/psum | solution.py:67
  143.0 1.3 fusion.19
  144.3 68.1 %fusion.63 = (f32[128]{0:T(128)S(1)}, f32[128,37984]{0,1:T(8,128)}) fusion(bf16[37984,2048]{1,0:T(8,128)(2,1)} %param.37, bf16[128,2048]{1,0:T(8,128)(2,1)S(1)} %get-tuple-element.12, f32[2048]{0:T(1024)S(1)} %convert_element_type.106, f32[128]{0:T(128)S(1)} %add_rsqrt_fusion), kind=kOutput, calls=%fused_computation.87 | convolution fusion | flops 19920465920 | bytes 175563776 | tf_op jit(solution)/shard_map/dot_general | solution.py:70
  212.5 9.5 %exponential_reduce_fusion = (f32[128]{0:T(128)S(1)}, f32[128]{0:T(128)S(1)}) fusion(f32[128,37984]{0,1:T(8,128)} %get-tuple-element.30, f32[128]{0:T(128)S(1)} %get-tuple-element.29, s32[128]{0:T(128)S(1)} %broadcast_subtract_fusion), kind=kLoop, calls=%fused_computation.3 | loop fusion | flops 24309504 | bytes 19449856 | tf_op jit(solution)/shard_map/reduce_sum | solution.py:75
  222.0 6.5 %all-gather.1 = f32[4,3,128]{2,1,0:T(4,128)S(1)} all-gather(f32[1,3,128]{2,1,0:T(4,128)S(1)} %maximum_bitcast_fusion), channel_id=2, replica_groups=mesh['dp'=2,'tp'=4] {'tp'}, dimensions={0}, use_global_device_ids=true | all-gather | bytes 7680 | tf_op jit(solution)/shard_map/all_gather | solution.py:77
  228.5 0.5 fusion.59
  (24 shorter events, 0.2 us)
Async XLA Ops:
  7.2 52.9 %copy-start = (bf16[512,2048]{1,0:T(8,128)(2,1)S(1)}, bf16[512,2048]{1,0:T(8,128)(2,1)}, u32[]{:S(2)}) copy-start(bf16[512,2048]{1,0:T(8,128)(2,1)} %param.31) | copy-start | bytes 6291460
  7.2 85.0 %all-reduce.3.cloned.1.call-start = ((), (), s32[]{:S(2)}) async-start(), calls=%async_computation | async-start | bytes 1048576 | tf_op jit(solution)/shard_map/psum | solution.py:60
  53.0 8.7 %copy-start.3 = (bf16[2048]{0:T(1024)(128)(2,1)S(1)}, bf16[2048]{0:T(1024)(128)(2,1)}, u32[]{:S(2)}) copy-start(bf16[2048]{0:T(1024)(128)(2,1)} %param.32) | copy-start | bytes 12292
  61.4 81.6 %all-reduce.5.cloned.1.call-start = ((), (), s32[]{:S(2)}) async-start(), calls=%async_computation.1 | async-start | bytes 1048576 | tf_op jit(solution)/shard_map/psum | solution.py:67
  99.7 15.4 %copy-start.4 = (bf16[2048]{0:T(1024)(128)(2,1)S(1)}, bf16[2048]{0:T(1024)(128)(2,1)}, u32[]{:S(2)}) copy-start(bf16[2048]{0:T(1024)(128)(2,1)} %param.36) | copy-start | bytes 12292
  99.7 15.4 %copy-start.5 = (s32[128]{0:T(128)S(1)}, s32[128]{0:T(128)}, u32[]{:S(2)}) copy-start(s32[128]{0:T(128)} %param.23) | copy-start | bytes 1540
  144.3 68.2 %copy-start.2 = (bf16[128,2048]{1,0:T(8,128)(2,1)}, bf16[128,2048]{1,0:T(8,128)(2,1)S(1)}, u32[]{:S(2)}) copy-start(bf16[128,2048]{1,0:T(8,128)(2,1)S(1)} %get-tuple-element.12) | copy-start | bytes 1572868
  144.3 84.7 %copy-start.1 = (bf16[512,2048]{1,0:T(8,128)(2,1)S(1)}, bf16[512,2048]{1,0:T(8,128)(2,1)}, u32[]{:S(2)}) copy-start(bf16[512,2048]{1,0:T(8,128)(2,1)} %param.31) | copy-start | bytes 6291460
Sparse Core Ops, SparseCore 0:
  61.5 30.5 all-reduce.2
  115.2 27.7 all-reduce.4
where the time goes:
time: 237 us; the launch traced here: 236 us
  matrix products  114 us (48%)
  waiting for transfers between devices  58.4 us (25%)
  other arithmetic  42.5 us (18%)
  between operations  14.2 us (6%)
  blocking collectives  6.46 us (3%)
    dot_general x1, matrix products, local_step(): lax.dot_general(final_norm, w_head, (((1,), (1,)), ((), ())), preferred_e...  68.1 us
    psum x1, waiting for transfers between devices, local_step(): attn_sum = lax.psum(attn_part, 'tp')  30.5 us
    psum x1, waiting for transfers between devices, local_step(): down_sum = lax.psum(down_part, 'tp')  27.9 us
    select_n x1, other arithmetic, attention_block(): k_all = jnp.where(write_mask, k_new[:, None], k_cache)  23.3 us
    dot_general x1, matrix products, local_step(): jnp.dot(hidden, w_down, preferred_element_type=jnp.float32)  15.4 us
    sub x1, matrix products, attention_block(): exp_scores = jnp.exp(scores - row_max)  10.4 us
    reduce_sum x1, other arithmetic, local_step(): local_sum = jnp.sum(jnp.exp(logits - local_max[:, None]), axis=1)  9.5 us
    dot_general x1, matrix products, attention_block(): jnp.einsum('bkgl,blkd->bkgd', attn_probs, v_all, preferred_element_type=j...  7.12 us
  transfers between devices with their start and end apart: 2, of which 2 were waited for; matrix products, arithmetic and copies ran while one was open for 0% of the time, Pallas kernels for 0%

commit v1 on v0

v1 whole, which is shorter than its diff:
```python
import jax
import jax.numpy as jnp
from jax import lax
from jax.experimental import pallas as pl
from jax.experimental.pallas import tpu as pltpu
from jax.sharding import PartitionSpec as P

THETA = 1000000.0
EPS = 1e-6
MESH = pl.DeviceIdType.MESH
F32 = jnp.float32
BF16 = jnp.bfloat16
VMEM_BYTES = 67043328

ROWS = 128
WIDTH = 2048
HEAD = 128
SLOTS = 512
GROUP = 32
CHUNK = 256
NCH = 8
HALF = 4
TILE = 768
RING = 18


def dot(a, b):
    return lax.dot_general(a, b, (((1,), (0,)), ((), ())), preferred_element_type=F32)


def dot_t(a, b):
    return lax.dot_general(a, b, (((1,), (1,)), ((), ())), preferred_element_type=F32)


def attn_kernel(lens_ref, x_ref, g_ref, cos_ref, sin_ref, lanelen_ref, bq_ref, bk_ref, bv_ref,
                wq_hbm, wk_hbm, wv_hbm, wo_hbm, k_hbm, v_hbm,
                part_ref, ko_hbm, vo_hbm,
                kbuf, vbuf, wq, wk, wv, wo, q_s, k_s, v_s, qg_s, qt_s, sc_s, pt_s, o_s, at_s,
                wsem, ksem, vsem, kosem, vosem):
    groups = ROWS // GROUP
    part = GROUP // 4
    for i, (src, dst) in enumerate(((wq_hbm, wq), (wk_hbm, wk), (wv_hbm, wv))):
        pltpu.make_async_copy(src, dst, wsem.at[i]).start()

    def start_in(g, hbm, buf, sem):
        for i in range(4):
            rows = pl.ds(g * GROUP + i * part, part)
            pltpu.make_async_copy(hbm.at[rows], buf.at[rows], sem.at[g]).start()

    for g in range(groups):
        start_in(g, k_hbm, kbuf, ksem)
        start_in(g, v_hbm, vbuf, vsem)
        if g == 0:
            pltpu.make_async_copy(wo_hbm, wo, wsem.at[3]).start()

    x = x_ref[...].astype(F32)
    inv = lax.rsqrt(jnp.mean(x * x, axis=-1, keepdims=True) + EPS)
    normed = (x * inv * g_ref[...].astype(F32)).astype(BF16)
    cos = cos_ref[...]
    sin = sin_ref[...]
    for i, (src, dst) in enumerate(((wq_hbm, wq), (wk_hbm, wk), (wv_hbm, wv))):
        pltpu.make_async_copy(src, dst, wsem.at[i]).wait()

    def rope(u):
        return u * cos + pltpu.roll(u, HEAD // 2, 1) * sin

    k_s[...] = rope(dot(normed, wk[...]) + bk_ref[...].astype(F32))
    v_s[...] = dot(normed, wv[...]) + bv_ref[...].astype(F32)
    for h in range(4):
        cols = slice(h * HEAD, (h + 1) * HEAD)
        q_s[h] = rope(dot(normed, wq[:, cols]) + bq_ref[:, cols].astype(F32))

    lane_seq = lax.broadcasted_iota(jnp.int32, (HEAD, 128), 1) // 4
    slot_id = lax.broadcasted_iota(jnp.int32, (SLOTS, 128), 0)
    row16 = lax.broadcasted_iota(jnp.int32, (16, HEAD), 0)
    row_seq = lax.broadcasted_iota(jnp.int32, (16, HEAD), 0) // 4

    def one_group(g, _):
        rows = pl.ds(pl.multiple_of(g * GROUP, GROUP), GROUP)
        pltpu.make_async_copy(k_hbm.at[rows], kbuf.at[rows], ksem.at[g]).wait()

        def put(new_s, buf):
            def one(i, _):
                b = g * GROUP + i
                length = lens_ref[b]
                base = pl.multiple_of((length // 16) * 16, 16)
                old = buf[b, pl.ds(base, 16), :]
                new = jnp.broadcast_to(new_s[pl.ds(b, 1), :].astype(BF16), (16, HEAD))
                buf[b, pl.ds(base, 16), :] = jnp.where(row16 == length - base, new, old)
                return 0
            lax.fori_loop(0, GROUP, one, 0, unroll=4)

        put(k_s, kbuf)
        for h in range(4):
            qg_s[pl.ds(h, GROUP, stride=4), :] = q_s[h, rows, :]
        qt_s[...] = qg_s[...].T.astype(BF16)
        qt = qt_s[...]
        zero = jnp.zeros_like(qt)
        acc = None
        for p in range(GROUP // 2):
            b = g * GROUP + 2 * p
            lhs = jnp.concatenate([kbuf[b], kbuf[b + 1]], axis=1)
            rhs = jnp.concatenate([jnp.where(lane_seq == 2 * p, qt, zero), jnp.where(lane_seq == 2 * p + 1, qt, zero)], axis=0)
            term = dot(lhs, rhs)
            acc = term if acc is None else acc + term
        sc_s[...] = acc
        pltpu.make_async_copy(kbuf.at[rows], ko_hbm.at[rows], kosem.at[g]).start()
        live = slot_id <= lanelen_ref[pl.ds(g, 1), :]
        scores = jnp.where(live, sc_s[...] * (HEAD ** -0.5), -jnp.inf)
        top = jnp.max(scores, axis=0, keepdims=True)
        exps = jnp.exp(scores - top)
        sc_s[...] = exps
        recip = 1.0 / jnp.sum(exps, axis=0, keepdims=True)
        for i in range(4):
            blk = sc_s[i * 128:(i + 1) * 128, :] * recip
            pt_s[:, i * 128:(i + 1) * 128] = blk.T.astype(BF16)

        pltpu.make_async_copy(v_hbm.at[rows], vbuf.at[rows], vsem.at[g]).wait()
        put(v_s, vbuf)
        for j in range(GROUP // 4):
            b = g * GROUP + 4 * j
            rhs = jnp.concatenate([vbuf[b + i] for i in range(4)], axis=1)
            out = dot(pt_s[16 * j:16 * j + 16, :], rhs)
            o = jnp.zeros((16, HEAD), F32)
            for i in range(4):
                o = jnp.where(row_seq == i, out[:, i * HEAD:(i + 1) * HEAD], o)
            o_s[16 * j:16 * j + 16, :] = o
        pltpu.make_async_copy(vbuf.at[rows], vo_hbm.at[rows], vosem.at[g]).start()
        for h in range(4):
            at_s[rows, h * HEAD:(h + 1) * HEAD] = o_s[pl.ds(h, GROUP, stride=4), :].astype(BF16)
        return 0

    lax.fori_loop(0, groups, one_group, 0)

    pltpu.make_async_copy(wo_hbm, wo, wsem.at[3]).wait()
    attn = at_s[...]
    for c in range(NCH):
        part_ref[c] = dot(attn, wo[:, c * CHUNK:(c + 1) * CHUNK]).astype(BF16)
    for g in range(groups):
        rows = pl.ds(g * GROUP, GROUP)
        pltpu.make_async_copy(kbuf.at[rows], ko_hbm.at[rows], kosem.at[g]).wait()
        pltpu.make_async_copy(vbuf.at[rows], vo_hbm.at[rows], vosem.at[g]).wait()


def tail_kernel(ff, vocab_loc,
                part_ref, x_ref, gm_ref, gf_ref, tok_ref, wg_hbm, wu_hbm, wd_hbm, wh_hbm,
                y_ref, logp_ref, lse_ref,
                wbuf, r1, s1, r2, a_s, m_s, hid, p2, r1b, s2, r2b, y_s, f_s, tok2, st_s, st_r,
                wsem, s_d1, r_d1, s_x1, r_x1, s_a, r_a, s_d2, r_d2, s_x2, r_x2,
                s_y, r_y, s_o, r_o, s_f, r_f, s_t, r_t, s_st, r_st):
    dp = lax.axis_index('dp')
    tp = lax.axis_index('tp')
    core = lax.rem(tp, 2)
    dev = dp * 4 + tp
    partner = (dp, tp + 1 - 2 * core)
    xnext = (dp, lax.rem(tp + 2, 4))
    ynext = (1 - dp, tp)
    mine = core * HALF
    other = (1 - core) * HALF

    mlp_tiles = [(i * TILE, min(TILE, ff - i * TILE)) for i in range(-(-ff // TILE))]
    n_mlp = len(mlp_tiles)
    tail_pad = -(-mlp_tiles[-1][1] // CHUNK) * CHUNK
    vocab_half = vocab_loc // 2
    n_full = vocab_half // TILE
    n_tail = vocab_half - n_full * TILE
    n_head = n_full + (1 if n_tail else 0)
    head0 = 3 * n_mlp
    vbase = dp * vocab_half

    def mlp_copy(i):
        if i < 2 * n_mlp:
            src, (r, n) = (wg_hbm, wu_hbm)[i % 2], mlp_tiles[i // 2]
        else:
            src, (r, n) = wd_hbm, mlp_tiles[i - 2 * n_mlp]
        slot = i % RING
        return pltpu.make_async_copy(src.at[pl.ds(r, n)], wbuf.at[slot, pl.ds(0, n)], wsem.at[slot])

    def head_copy(i, n=TILE):
        slot = lax.rem(head0 + i, RING)
        start = pl.multiple_of(vbase + i * TILE, 16)
        return pltpu.make_async_copy(wh_hbm.at[pl.ds(start, n)], wbuf.at[slot, pl.ds(0, n)], wsem.at[slot])

    def start_item(i):
        if i < head0:
            mlp_copy(i).start()
        elif i - head0 < n_full:
            head_copy(i - head0).start()
        elif i - head0 < n_head:
            head_copy(i - head0, n_tail).start()

    for i in range(RING):
        start_item(i)

    barrier = pltpu.get_barrier_semaphore()
    for d in range(2):
        for t in range(4):
            @pl.when(d * 4 + t != dev)
            def _():
                pl.semaphore_signal(barrier, inc=1, device_id=(d, t), device_id_type=MESH)
    last_n = mlp_tiles[-1][1]
    if tail_pad > last_n:
        for i in (2 * n_mlp - 2, 2 * n_mlp - 1, 3 * n_mlp - 1):
            wbuf[i % RING, last_n:tail_pad, :] = jnp.zeros((tail_pad - last_n, WIDTH), BF16)
    pl.semaphore_wait(barrier, 7)

    def remote(src, dst, ssem, rsem, who):
        return pltpu.make_async_remote_copy(src_ref=src, dst_ref=dst, send_sem=ssem, recv_sem=rsem, device_id=who, device_id_type=MESH)

    tok_copy = remote(tok_ref, tok2, s_t, r_t, ynext)
    d1 = [remote(part_ref.at[other + j], r1.at[j], s_d1.at[j], r_d1.at[j], partner) for j in range(HALF)]
    x1 = [remote(s1.at[j], r2.at[j], s_x1.at[j], r_x1.at[j], xnext) for j in range(HALF)]
    ac = [remote(a_s.at[mine + j], a_s.at[mine + j], s_a.at[j], r_a.at[j], partner) for j in range(HALF)]
    d2 = [remote(p2.at[other + j], r1b.at[j], s_d2.at[j], r_d2.at[j], partner) for j in range(HALF)]
    x2 = [remote(s2.at[j], r2b.at[j], s_x2.at[j], r_x2.at[j], xnext) for j in range(HALF)]
    yo = [remote(y_s.at[0, mine + j], y_s.at[0, mine + j], s_o.at[j], r_o.at[j], partner) for j in range(HALF)]
    yy = [remote(y_s.at[0, mine + j], y_s.at[1, mine + j], s_y.at[j], r_y.at[j], ynext) for j in range(HALF)]
    yf = [remote(y_s.at[1, mine + j], y_s.at[1, mine + j], s_f.at[j], r_f.at[j], partner) for j in range(HALF)]

    def cols_of(c):
        return pl.ds(pl.multiple_of(c * CHUNK, CHUNK), CHUNK)

    for j in range(HALF):
        d1[j].start()
    tok_copy.start()
    for j in range(HALF):
        d1[j].wait_recv()
        s1[j] = (part_ref[mine + j].astype(F32) + r1[j].astype(F32)).astype(BF16)
        x1[j].start()
    for j in range(HALF):
        x1[j].wait_recv()
        total = s1[j].astype(F32) + r2[j].astype(F32)
        a_s[mine + j] = (x_ref[:, cols_of(mine + j)].astype(F32) + total).astype(BF16)
        ac[j].start()
    for j in range(HALF):
        ac[j].wait_recv()

    def inv_rms(src):
        total = jnp.zeros((ROWS, CHUNK), F32)
        for c in range(NCH):
            v = src[c].astype(F32)
            total = total + v * v
        return lax.rsqrt(jnp.sum(total, axis=-1, keepdims=True) * (1.0 / WIDTH) + EPS)

    inv = inv_rms(a_s)
    for c in range(NCH):
        cols = slice(c * CHUNK, (c + 1) * CHUNK)
        m_s[:, cols] = (a_s[c].astype(F32) * inv * gm_ref[:, cols].astype(F32)).astype(BF16)

    for i, (r, n) in enumerate(mlp_tiles):
        mlp_copy(2 * i).wait()
        mlp_copy(2 * i + 1).wait()
        gslot, uslot = (2 * i) % RING, (2 * i + 1) % RING
        pad = -(-n // CHUNK) * CHUNK
        for b in range(0, pad, CHUNK):
            gate = dot_t(m_s[...], wbuf[gslot, b:b + CHUNK, :])
            up = dot_t(m_s[...], wbuf[uslot, b:b + CHUNK, :])
            hid[:, r + b:r + b + CHUNK] = (gate * jax.nn.sigmoid(gate) * up).astype(BF16)
        start_item(2 * i + RING)
        start_item(2 * i + 1 + RING)

    for i in range(n_mlp):
        mlp_copy(2 * n_mlp + i).wait()

    def down(c):
        acc = None
        for i, (r, n) in enumerate(mlp_tiles):
            pad = -(-n // CHUNK) * CHUNK
            term = dot(hid[:, r:r + pad], wbuf[(2 * n_mlp + i) % RING, :pad, cols_of(c)])
            acc = term if acc is None else acc + term
        return acc.astype(BF16)

    def chip_sum(j):
        d2[j].wait_recv()
        s2[j] = (p2[mine + j].astype(F32) + r1b[j].astype(F32)).astype(BF16)
        x2[j].start()

    for j in range(HALF):
        p2[other + j] = down(other + j)
        d2[j].start()
        p2[mine + j] = down(mine + j)
        if j:
            chip_sum(j - 1)
    chip_sum(HALF - 1)
    for i in range(n_mlp):
        start_item(2 * n_mlp + i + RING)

    def forward(j):
        yy[j].wait_recv()
        yf[j].start()

    for j in range(HALF):
        x2[j].wait_recv()
        total = s2[j].astype(F32) + r2b[j].astype(F32)
        y_s[0, mine + j] = (a_s[mine + j].astype(F32) + total).astype(BF16)
        yy[j].start()
        yo[j].start()
        if j:
            forward(j - 1)
    forward(HALF - 1)
    for j in range(HALF):
        yo[j].wait_recv()
    for c in range(NCH):
        y_ref[:, c * CHUNK:(c + 1) * CHUNK] = y_s[0, c]

    def final_norm(grp):
        inv = inv_rms(y_s.at[grp])
        for c in range(NCH):
            cols = slice(c * CHUNK, (c + 1) * CHUNK)
            f_s[grp * ROWS:(grp + 1) * ROWS, cols] = (y_s[grp, c].astype(F32) * inv * gf_ref[:, cols].astype(F32)).astype(BF16)

    final_norm(0)
    for j in range(HALF):
        yf[j].wait_recv()
    final_norm(1)
    tok_copy.wait()

    tok = jnp.concatenate([tok_ref[...], tok2[...]], axis=1) - (tp * vocab_loc + vbase)
    row_id = lax.broadcasted_iota(jnp.int32, (8, 2 * ROWS), 0)

    def score(slot, first, n, state):
        top, tot, tgt = state
        for b in range(0, n, CHUNK):
            size = min(CHUNK, n - b)
            logits = dot_t(wbuf[slot, pl.ds(b, size), :], f_s[...])
            blocks = [logits[8 * i:8 * i + 8] for i in range(size // 8)]
            peak = blocks[0]
            for v in blocks[1:]:
                peak = jnp.maximum(peak, v)
            new = jnp.maximum(top, peak)
            part_sum = None
            for i, v in enumerate(blocks):
                e = jnp.exp(v - new)
                part_sum = e if part_sum is None else part_sum + e
                tgt = jnp.where(row_id + (first + b + 8 * i) == tok, v, tgt)
            tot = tot * jnp.exp(top - new) + part_sum
            top = new
        return top, tot, tgt

    def one_tile(i, state):
        slot = lax.rem(head0 + i, RING)
        head_copy(i).wait()
        state = score(slot, i * TILE, TILE, state)

        @pl.when(i + RING < n_full)
        def _():
            head_copy(i + RING).start()
        if n_tail:
            @pl.when(i + RING == n_full)
            def _():
                head_copy(n_full, n_tail).start()
        return state

    state = (jnp.full((8, 2 * ROWS), -1e30, F32), jnp.zeros((8, 2 * ROWS), F32), jnp.zeros((8, 2 * ROWS), F32))
    state = lax.fori_loop(0, n_full, one_tile, state)
    if n_tail:
        head_copy(n_full, n_tail).wait()
        state = score((head0 + n_full) % RING, n_full * TILE, n_tail, state)
    top, tot, tgt = state
    peak = jnp.max(top, axis=0, keepdims=True)
    tot = jnp.sum(tot * jnp.exp(top - peak), axis=0, keepdims=True)
    tgt = jnp.sum(tgt, axis=0, keepdims=True)
    pad = jnp.zeros((5, ROWS), F32)
    for g in range(2):
        cols = slice(g * ROWS, (g + 1) * ROWS)
        st_s[g] = jnp.concatenate([peak[:, cols], tot[:, cols], tgt[:, cols], pad], axis=0)

    sends = []
    for k in range(1, 8):
        who = lax.rem(dev + k, 8)
        whod, whot = who // 4, lax.rem(who, 4)
        grp = lax.rem(whod + dp, 2)
        sends.append(remote(st_s.at[grp], st_r.at[dev], s_st.at[k - 1], r_st.at[k - 1], (whod, whot)))
    for c in sends:
        c.start()
    st_r[dev] = st_s[0]
    for c in sends:
        c.wait()
    stats = [st_r[i] for i in range(8)]
    peak = stats[0][0:1]
    for s in stats[1:]:
        peak = jnp.maximum(peak, s[0:1])
    tot = jnp.zeros_like(peak)
    tgt = jnp.zeros_like(peak)
    for s in stats:
        tot = tot + s[1:2] * jnp.exp(s[0:1] - peak)
        tgt = tgt + s[2:3]
    lse = peak + jnp.log(tot)
    lse_ref[...] = lse
    logp_ref[...] = tgt - lse

    for group in (d1, x1, ac, d2, x2, yo, yy, yf):
        for c in group:
            c.wait_send()


def local_step(tok_hidden, seq_lens, k_cache, v_cache, next_tok, g_attn, w_q, b_q, w_k, b_k, w_v, b_v, w_o, g_mlp, w_gate, w_up, w_down, g_final, w_head):
    half = HEAD // 2
    inv_freq = jnp.power(THETA, jnp.arange(half, dtype=F32) * (-2.0 / HEAD))
    angles = seq_lens.astype(F32)[:, None] * inv_freq[None, :]
    cos, sin = jnp.cos(angles), jnp.sin(angles)
    cos_full = jnp.concatenate([cos, cos], axis=1)
    sin_full = jnp.concatenate([-sin, sin], axis=1)
    lane_len = jnp.repeat(seq_lens, 4).reshape(ROWS // GROUP, 128)
    vm = pl.BlockSpec(memory_space=pltpu.VMEM)
    sm = pl.BlockSpec(memory_space=pltpu.SMEM)
    hb = pl.BlockSpec(memory_space=pl.ANY)
    dma = pltpu.SemaphoreType.DMA
    cache = jax.ShapeDtypeStruct((ROWS, SLOTS, HEAD), BF16)
    part, k_all, v_all = pl.pallas_call(
        attn_kernel,
        out_shape=(jax.ShapeDtypeStruct((NCH, ROWS, CHUNK), BF16), cache, cache),
        in_specs=[sm] + [vm] * 8 + [hb] * 6,
        out_specs=(vm, hb, hb),
        scratch_shapes=[
            pltpu.VMEM((ROWS, SLOTS, HEAD), BF16), pltpu.VMEM((ROWS, SLOTS, HEAD), BF16),
            pltpu.VMEM((WIDTH, 512), BF16), pltpu.VMEM((WIDTH, HEAD), BF16), pltpu.VMEM((WIDTH, HEAD), BF16), pltpu.VMEM((512, WIDTH), BF16),
            pltpu.VMEM((4, ROWS, HEAD), F32), pltpu.VMEM((ROWS, HEAD), F32), pltpu.VMEM((ROWS, HEAD), F32),
            pltpu.VMEM((128, HEAD), F32), pltpu.VMEM((HEAD, 128), BF16), pltpu.VMEM((SLOTS, 128), F32), pltpu.VMEM((128, SLOTS), BF16),
            pltpu.VMEM((128, HEAD), F32), pltpu.VMEM((ROWS, 512), BF16),
            dma((4,)), dma((4,)), dma((4,)), dma((4,)), dma((4,)),
        ],
        compiler_params=pltpu.CompilerParams(vmem_limit_bytes=VMEM_BYTES),
        name="attention",
    )(seq_lens, tok_hidden, g_attn.reshape(1, WIDTH), cos_full, sin_full, lane_len, b_q.reshape(1, 512), b_k.reshape(1, HEAD), b_v.reshape(1, HEAD),
      w_q, w_k, w_v, w_o, k_cache.reshape(ROWS, SLOTS, HEAD), v_cache.reshape(ROWS, SLOTS, HEAD))

    ff = w_gate.shape[1]
    vocab_loc = w_head.shape[0]
    ff_pad = -(-ff // CHUNK) * CHUNK
    chunk4 = pltpu.VMEM((HALF, ROWS, CHUNK), BF16)
    chunk8 = pltpu.VMEM((NCH, ROWS, CHUNK), BF16)

    def kernel(*refs):
        tail_kernel(ff, vocab_loc, *refs)

    y_out, logp, lse = pl.pallas_call(
        kernel,
        out_shape=(jax.ShapeDtypeStruct((ROWS, WIDTH), BF16), jax.ShapeDtypeStruct((1, ROWS), F32), jax.ShapeDtypeStruct((1, ROWS), F32)),
        in_specs=[vm] * 5 + [hb] * 4,
        out_specs=(vm, vm, vm),
        scratch_shapes=[
            pltpu.VMEM((RING, TILE, WIDTH), BF16),
            chunk4, chunk4, chunk4, chunk8, pltpu.VMEM((ROWS, WIDTH), BF16), pltpu.VMEM((ROWS, ff_pad), BF16),
            chunk8, chunk4, chunk4, chunk4, pltpu.VMEM((2, NCH, ROWS, CHUNK), BF16), pltpu.VMEM((2 * ROWS, WIDTH), BF16),
            pltpu.VMEM((1, ROWS), jnp.int32), pltpu.VMEM((2, 8, ROWS), F32), pltpu.VMEM((8, 8, ROWS), F32),
            dma((RING,)),
        ] + [dma((HALF,))] * 16 + [dma, dma, dma((7,)), dma((7,))],
        compiler_params=pltpu.CompilerParams(vmem_limit_bytes=VMEM_BYTES, collective_id=0, has_side_effects=True),
        name="tail",
    )(part, tok_hidden, g_mlp.reshape(1, WIDTH), g_final.reshape(1, WIDTH), next_tok.reshape(1, ROWS), w_gate.T, w_up.T, w_down, w_head)
    shape = (ROWS, SLOTS, 1, HEAD)
    return y_out, k_all.reshape(shape), v_all.reshape(shape), logp.reshape(ROWS), lse.reshape(ROWS)


def solution(mesh):
    row_spec = P('dp', None)
    vec_spec = P('dp')
    cache_spec = P('dp', None, 'tp', None)
    col_spec = P(None, 'tp')
    part_spec = P('tp')
    whole_spec = P(None)
    in_specs = (row_spec, vec_spec, cache_spec, cache_spec, vec_spec, whole_spec, col_spec, part_spec, col_spec, part_spec, col_spec, part_spec, P('tp', None), whole_spec, col_spec, col_spec, P('tp', None), whole_spec, P('tp', None))
    out_specs = (row_spec, cache_spec, cache_spec, vec_spec, vec_spec)
    return jax.shard_map(local_step, mesh=mesh, in_specs=in_specs, out_specs=out_specs, check_vma=False)
```

time: 237 us -> 113 us (0.48)
  matrix products: 114 us -> 0 us
  Pallas kernels: 0 us -> 99.9 us
  waiting for transfers between devices: 58.4 us -> 0 us
  other arithmetic: 42.5 us -> 1.73 us
  between operations: 14.2 us -> 0.66 us
  local copies, waits for them, and re-layouts: 0.24 us -> 10.8 us
  blocking collectives: 6.46 us -> 0 us
    dot_general x8 -> x0, matrix products: 103 us -> none  [the longest x1 68.1 us: local_step(): lax.dot_general(final_norm, w_head, (((1,), (1,)), ((), ())), preferred_e...]
    pallas_call x0 -> x2, Pallas kernels: none -> 99.9 us  [the longest x1 70.2 us: local_step(): pl.pallas_call(kernel, out_shape=(jax.ShapeDtypeStruct((ROWS, WIDTH), BF1...]
    psum x2 -> x0, waiting for transfers between devices: 58.4 us -> none  [the longest x1 30.5 us: local_step(): attn_sum = lax.psum(attn_part, 'tp')]
    select_n x1 -> x0, other arithmetic: 23.3 us -> none  [attention_block(): k_all = jnp.where(write_mask, k_new[:, None], k_cache)]
    reduce_sum x5 -> x0, other arithmetic: 13.5 us -> none  [the longest x1 9.5 us: local_step(): local_sum = jnp.sum(jnp.exp(logits - local_max[:, None]), axis=1)]
    sub x1 -> x0, matrix products: 10.4 us -> none  [attention_block(): exp_scores = jnp.exp(scores - row_max)]
    all_gather x1 -> x0, blocking collectives: 6.46 us -> none  [local_step(): lax.all_gather(jnp.stack([local_max, local_sum, local_target]), 'tp')]
    reshape x1 -> x4, local copies, waits for them, and re-layouts: 0.09 us -> 5.1 us  [the longest x1 1.29 us: local_step(): g_mlp.reshape(1, WIDTH)]
  transfers between devices with their start and end apart: 2 -> 0, of which waited for: 2 -> 0; matrix products, arithmetic and copies ran while one was open for 0% -> 0% of each run, Pallas kernels for 0% -> 0%
where the time goes in v1:
time: 113 us
  Pallas kernels  99.9 us (88%)
  local copies, waits for them, and re-layouts  10.8 us (10%)
  other arithmetic  1.73 us (2%)
    pallas_call x1, Pallas kernels, local_step(): pl.pallas_call(kernel, out_shape=(jax.ShapeDtypeStruct((ROWS, WIDTH), BF1...  70.2 us
    pallas_call x1, Pallas kernels, local_step(): pl.pallas_call(attn_kernel, out_shape=(jax.ShapeDtypeStruct((NCH, ROWS, C...  29.6 us
    unnamed x3, local copies, waits for them, and re-layouts  4.16 us

profile of v1, /device:TPU:0, one launch (start us, length us, event | category | flops | bytes accessed | tf_op | source)
XLA Modules:
  0.0 113.0 jit_solution(1351015340191659164)
XLA Ops:
  0.6 0.7 convert_element_type.3
  1.3 1.2 %reshape.58.bq_ref = bf16[1,512]{1,0:T(2,128)(2,1)} reshape(bf16[512]{0:T(512)(128)(2,1)} %param.26) | data formatting | bytes 2048 | tf_op jit(solution)/shard_map/reshape | solution.py:425
  2.5 0.7 broadcast_in_dim.9
  3.3 1.3 %reshape.57.g_ref = bf16[1,2048]{1,0:T(2,128)(2,1)} reshape(bf16[2048]{0:T(1024)(128)(2,1)} %param.24) | data formatting | bytes 8192 | tf_op jit(solution)/shard_map/reshape | solution.py:425
  4.6 1.3 %reshape.63.refs_2_ = bf16[1,2048]{1,0:T(2,128)(2,1)} reshape(bf16[2048]{0:T(1024)(128)(2,1)} %param.32) | data formatting | bytes 8192 | tf_op jit(solution)/shard_map/reshape | solution.py:451
  5.9 1.3 %reshape.64.refs_3_ = bf16[1,2048]{1,0:T(2,128)(2,1)} reshape(bf16[2048]{0:T(1024)(128)(2,1)} %param.36) | data formatting | bytes 8192 | tf_op jit(solution)/shard_map/reshape | solution.py:451
  7.1 0.1 broadcast_in_dim.10
  7.2 0.7 broadcast_in_dim.11.lanelen_ref
  7.9 0.3 fusion
  8.2 0.8 pad_maximum_fusion
  9.0 29.6 %attention.1 = (bf16[8,128,256]{2,1,0:T(8,128)(2,1)}, bf16[128,512,128]{2,1,0:T(8,128)(2,1)}, bf16[128,512,128]{2,1,0:T(8,128)(2,1)}) custom-call(s32[128]{0:T(128)} %lens_ref.1, bf16[128,2048]{1,0:T(8,128)(2,1)} %refs_1_.1, bf16[1,2048]{1,0:T(2,128)(2,1)} %reshape.57.g_ref, f32[128,128]{1,0:T(8,128)} %get-tuple-element.30.cos_ref, ...), custom_call_target="tpu_custom_call" | custom-call | tf_op jit(solution)/shard_map/attention/pallas_call | solution.py:410
  38.6 70.2 %tail.1 = (bf16[128,2048]{1,0:T(8,128)(2,1)}, f32[1,128]{1,0:T(1,128)}, f32[1,128]{1,0:T(1,128)}) custom-call(bf16[8,128,256]{2,1,0:T(8,128)(2,1)} %get-tuple-element.11.refs_0_, bf16[128,2048]{1,0:T(8,128)(2,1)} %refs_1_.1, bf16[1,2048]{1,0:T(2,128)(2,1)} %reshape.63.refs_2_, bf16[1,2048]{1,0:T(2,128)(2,1)} %reshape.64.refs_3_, s32[1,128]{1,0:T(1,128)} %bitcast.19, ...), custom_call_target="tpu_custom_call" | custom-call | tf_op jit(solution)/shard_map/tail/pallas_call | solution.py:437
  108.8 1.9 %copy.31 = bf16[128,2048]{1,0:T(8,128)(2,1)} copy(bf16[128,2048]{1,0:T(8,128)(2,1)} %get-tuple-element.37) | data formatting | bytes 1048576
  110.7 1.2 %copy.32 = f32[128]{0:T(128)} copy(f32[128]{0:T(128)} %bitcast.25) | data formatting | bytes 1024
  111.9 1.1 copy.33
  (1 shorter events, 0.0 us)

commit v2 on v1

--- a/solution.py
+++ b/solution.py
@@ -1,4 +1,5 @@
 import jax
+import numpy as np
 import jax.numpy as jnp
 from jax import lax
 from jax.experimental import pallas as pl
@@ -32,13 +33,18 @@
     return lax.dot_general(a, b, (((1,), (1,)), ((), ())), preferred_element_type=F32)
 
 
-def attn_kernel(lens_ref, x_ref, g_ref, cos_ref, sin_ref, lanelen_ref, bq_ref, bk_ref, bv_ref,
+def attn_kernel(lens_ref, lenv_hbm, freq_hbm, x_hbm, g_hbm, bq_hbm, bk_hbm, bv_hbm,
                 wq_hbm, wk_hbm, wv_hbm, wo_hbm, k_hbm, v_hbm,
                 part_ref, ko_hbm, vo_hbm,
-                kbuf, vbuf, wq, wk, wv, wo, q_s, k_s, v_s, qg_s, qt_s, sc_s, pt_s, o_s, at_s,
-                wsem, ksem, vsem, kosem, vosem):
+                lenv_ref, freq_ref, x_ref, g_ref, bq_ref, bk_ref, bv_ref,
+                kbuf, vbuf, wq, wk, wv, wo, q_s, k_s, v_s, qg_s, qt_s, sc_s, pt_s, o_s, at_s, ll_s,
+                wsem, ksem, vsem, kosem, vosem, insem):
     groups = ROWS // GROUP
     part = GROUP // 4
+    small = [pltpu.make_async_copy(src, dst, insem.at[i]) for i, (src, dst) in enumerate((
+        (x_hbm, x_ref), (lenv_hbm, lenv_ref), (freq_hbm, freq_ref), (g_hbm, g_ref), (bq_hbm, bq_ref), (bk_hbm, bk_ref), (bv_hbm, bv_ref)))]
+    for c in small:
+        c.start()
     for i, (src, dst) in enumerate(((wq_hbm, wq), (wk_hbm, wk), (wv_hbm, wv))):
         pltpu.make_async_copy(src, dst, wsem.at[i]).start()
 
@@ -53,22 +59,31 @@
         if g == 0:
             pltpu.make_async_copy(wo_hbm, wo, wsem.at[3]).start()
 
+    for c in small:
+        c.wait()
+    len_rows = jnp.broadcast_to(lenv_ref[...].astype(F32), (ROWS, ROWS)).T
+    angles = len_rows * freq_ref[...]
+    cos = jnp.cos(angles)
+    sin = jnp.sin(angles) * jnp.where(lax.broadcasted_iota(jnp.int32, (ROWS, HEAD), 1) < HEAD // 2, -1.0, 1.0)
+    seq_of = lax.broadcasted_iota(jnp.int32, (GROUP, 128), 1) // 4
+    pick = lax.broadcasted_iota(jnp.int32, (GROUP, 128), 0) == seq_of
+    for g in range(groups):
+        ll_s[g:g + 1, :] = jnp.sum(jnp.where(pick, len_rows[g * GROUP:(g + 1) * GROUP], 0.0), axis=0, keepdims=True).astype(jnp.int32)
+
     x = x_ref[...].astype(F32)
     inv = lax.rsqrt(jnp.mean(x * x, axis=-1, keepdims=True) + EPS)
-    normed = (x * inv * g_ref[...].astype(F32)).astype(BF16)
-    cos = cos_ref[...]
-    sin = sin_ref[...]
+    normed = (x * inv * g_ref[...].astype(F32).reshape(1, WIDTH)).astype(BF16)
     for i, (src, dst) in enumerate(((wq_hbm, wq), (wk_hbm, wk), (wv_hbm, wv))):
         pltpu.make_async_copy(src, dst, wsem.at[i]).wait()
 
     def rope(u):
         return u * cos + pltpu.roll(u, HEAD // 2, 1) * sin
 
-    k_s[...] = rope(dot(normed, wk[...]) + bk_ref[...].astype(F32))
-    v_s[...] = dot(normed, wv[...]) + bv_ref[...].astype(F32)
+    k_s[...] = rope(dot(normed, wk[...]) + bk_ref[...].astype(F32).reshape(1, HEAD))
+    v_s[...] = dot(normed, wv[...]) + bv_ref[...].astype(F32).reshape(1, HEAD)
+    q_all = dot(normed, wq[...]) + bq_ref[...].astype(F32).reshape(1, 4 * HEAD)
     for h in range(4):
-        cols = slice(h * HEAD, (h + 1) * HEAD)
-        q_s[h] = rope(dot(normed, wq[:, cols]) + bq_ref[:, cols].astype(F32))
+        q_s[h] = rope(q_all[:, h * HEAD:(h + 1) * HEAD])
 
     lane_seq = lax.broadcasted_iota(jnp.int32, (HEAD, 128), 1) // 4
     slot_id = lax.broadcasted_iota(jnp.int32, (SLOTS, 128), 0)
@@ -96,16 +111,18 @@
         qt_s[...] = qg_s[...].T.astype(BF16)
         qt = qt_s[...]
         zero = jnp.zeros_like(qt)
-        acc = None
+        top_half, low_half = None, None
         for p in range(GROUP // 2):
             b = g * GROUP + 2 * p
-            lhs = jnp.concatenate([kbuf[b], kbuf[b + 1]], axis=1)
             rhs = jnp.concatenate([jnp.where(lane_seq == 2 * p, qt, zero), jnp.where(lane_seq == 2 * p + 1, qt, zero)], axis=0)
-            term = dot(lhs, rhs)
-            acc = term if acc is None else acc + term
-        sc_s[...] = acc
+            t0 = dot(jnp.concatenate([kbuf[b, :SLOTS // 2], kbuf[b + 1, :SLOTS // 2]], axis=1), rhs)
+            t1 = dot(jnp.concatenate([kbuf[b, SLOTS // 2:], kbuf[b + 1, SLOTS // 2:]], axis=1), rhs)
+            top_half = t0 if top_half is None else top_half + t0
+            low_half = t1 if low_half is None else low_half + t1
+        sc_s[:SLOTS // 2] = top_half
+        sc_s[SLOTS // 2:] = low_half
         pltpu.make_async_copy(kbuf.at[rows], ko_hbm.at[rows], kosem.at[g]).start()
-        live = slot_id <= lanelen_ref[pl.ds(g, 1), :]
+        live = slot_id <= ll_s[pl.ds(g, 1), :]
         scores = jnp.where(live, sc_s[...] * (HEAD ** -0.5), -jnp.inf)
         top = jnp.max(scores, axis=0, keepdims=True)
         exps = jnp.exp(scores - top)
@@ -119,11 +136,12 @@
         put(v_s, vbuf)
         for j in range(GROUP // 4):
             b = g * GROUP + 4 * j
-            rhs = jnp.concatenate([vbuf[b + i] for i in range(4)], axis=1)
-            out = dot(pt_s[16 * j:16 * j + 16, :], rhs)
+            probs = pt_s[16 * j:16 * j + 16, :]
             o = jnp.zeros((16, HEAD), F32)
-            for i in range(4):
-                o = jnp.where(row_seq == i, out[:, i * HEAD:(i + 1) * HEAD], o)
+            for i in range(0, 4, 2):
+                out = dot(probs, jnp.concatenate([vbuf[b + i], vbuf[b + i + 1]], axis=1))
+                o = jnp.where(row_seq == i, out[:, :HEAD], o)
+                o = jnp.where(row_seq == i + 1, out[:, HEAD:], o)
             o_s[16 * j:16 * j + 16, :] = o
         pltpu.make_async_copy(vbuf.at[rows], vo_hbm.at[rows], vosem.at[g]).start()
         for h in range(4):
@@ -143,11 +161,11 @@
 
 
 def tail_kernel(ff, vocab_loc,
-                part_ref, x_ref, gm_ref, gf_ref, tok_ref, wg_hbm, wu_hbm, wd_hbm, wh_hbm,
+                part_hbm, x_hbm, gm_hbm, gf_hbm, tok_hbm, wg_hbm, wu_hbm, wd_hbm, wh_hbm,
                 y_ref, logp_ref, lse_ref,
-                wbuf, r1, s1, r2, a_s, m_s, hid, p2, r1b, s2, r2b, y_s, f_s, tok2, st_s, st_r,
+                part_ref, x_ref, gm_ref, gf_ref, tok_ref, wbuf, r1, s1, r2, a_s, m_s, hid, p2, r1b, s2, r2b, y_s, f_s, tok2, st_s, st_r,
                 wsem, s_d1, r_d1, s_x1, r_x1, s_a, r_a, s_d2, r_d2, s_x2, r_x2,
-                s_y, r_y, s_o, r_o, s_f, r_f, s_t, r_t, s_st, r_st):
+                s_y, r_y, s_o, r_o, s_f, r_f, s_t, r_t, s_st, r_st, insem):
     dp = lax.axis_index('dp')
     tp = lax.axis_index('tp')
     core = lax.rem(tp, 2)
@@ -189,6 +207,10 @@
         elif i - head0 < n_head:
             head_copy(i - head0, n_tail).start()
 
+    small = [pltpu.make_async_copy(src, dst, insem.at[i]) for i, (src, dst) in enumerate((
+        (part_hbm, part_ref), (x_hbm, x_ref), (gm_hbm, gm_ref), (gf_hbm, gf_ref), (tok_hbm, tok_ref)))]
+    for c in small:
+        c.start()
     for i in range(RING):
         start_item(i)
 
@@ -202,6 +224,8 @@
     if tail_pad > last_n:
         for i in (2 * n_mlp - 2, 2 * n_mlp - 1, 3 * n_mlp - 1):
             wbuf[i % RING, last_n:tail_pad, :] = jnp.zeros((tail_pad - last_n, WIDTH), BF16)
+    for c in small:
+        c.wait()
     pl.semaphore_wait(barrier, 7)
 
     def remote(src, dst, ssem, rsem, who):
@@ -243,9 +267,10 @@
         return lax.rsqrt(jnp.sum(total, axis=-1, keepdims=True) * (1.0 / WIDTH) + EPS)
 
     inv = inv_rms(a_s)
+    gm = gm_ref[...].astype(F32).reshape(1, WIDTH)
     for c in range(NCH):
         cols = slice(c * CHUNK, (c + 1) * CHUNK)
-        m_s[:, cols] = (a_s[c].astype(F32) * inv * gm_ref[:, cols].astype(F32)).astype(BF16)
+        m_s[:, cols] = (a_s[c].astype(F32) * inv * gm[:, cols]).astype(BF16)
 
     for i, (r, n) in enumerate(mlp_tiles):
         mlp_copy(2 * i).wait()
@@ -276,9 +301,10 @@
         x2[j].start()
 
     for j in range(HALF):
-        p2[other + j] = down(other + j)
+        theirs, ours = down(other + j), down(mine + j)
+        p2[other + j] = theirs
+        p2[mine + j] = ours
         d2[j].start()
-        p2[mine + j] = down(mine + j)
         if j:
             chip_sum(j - 1)
     chip_sum(HALF - 1)
@@ -303,11 +329,13 @@
     for c in range(NCH):
         y_ref[:, c * CHUNK:(c + 1) * CHUNK] = y_s[0, c]
 
+    gf = gf_ref[...].astype(F32).reshape(1, WIDTH)
+
     def final_norm(grp):
         inv = inv_rms(y_s.at[grp])
         for c in range(NCH):
             cols = slice(c * CHUNK, (c + 1) * CHUNK)
-            f_s[grp * ROWS:(grp + 1) * ROWS, cols] = (y_s[grp, c].astype(F32) * inv * gf_ref[:, cols].astype(F32)).astype(BF16)
+            f_s[grp * ROWS:(grp + 1) * ROWS, cols] = (y_s[grp, c].astype(F32) * inv * gf[:, cols]).astype(BF16)
 
     final_norm(0)
     for j in range(HALF):
@@ -320,8 +348,8 @@
 
     def score(slot, first, n, state):
         top, tot, tgt = state
-        for b in range(0, n, CHUNK):
-            size = min(CHUNK, n - b)
+        cut = -(-n // 32) * 16
+        for b, size in ((0, cut), (cut, n - cut)):
             logits = dot_t(wbuf[slot, pl.ds(b, size), :], f_s[...])
             blocks = [logits[8 * i:8 * i + 8] for i in range(size // 8)]
             peak = blocks[0]
@@ -394,35 +422,38 @@
             c.wait_send()
 
 
+def emit_kernel(y_in, logp_in, lse_in, y_out, logp_out, lse_out):
+    y_out[...] = y_in[...]
+    logp_out[...] = logp_in[...]
+    lse_out[...] = lse_in[...]
+
+
 def local_step(tok_hidden, seq_lens, k_cache, v_cache, next_tok, g_attn, w_q, b_q, w_k, b_k, w_v, b_v, w_o, g_mlp, w_gate, w_up, w_down, g_final, w_head):
-    half = HEAD // 2
-    inv_freq = jnp.power(THETA, jnp.arange(half, dtype=F32) * (-2.0 / HEAD))
-    angles = seq_lens.astype(F32)[:, None] * inv_freq[None, :]
-    cos, sin = jnp.cos(angles), jnp.sin(angles)
-    cos_full = jnp.concatenate([cos, cos], axis=1)
-    sin_full = jnp.concatenate([-sin, sin], axis=1)
-    lane_len = jnp.repeat(seq_lens, 4).reshape(ROWS // GROUP, 128)
+    steps = np.arange(HEAD // 2, dtype=np.float32) * np.float32(-2.0 / HEAD)
+    freq = jnp.asarray(np.tile(np.power(np.float64(THETA), steps.astype(np.float64)).astype(np.float32), 2)[None])
     vm = pl.BlockSpec(memory_space=pltpu.VMEM)
     sm = pl.BlockSpec(memory_space=pltpu.SMEM)
-    hb = pl.BlockSpec(memory_space=pl.ANY)
+    hb = pl.BlockSpec(memory_space=pltpu.HBM)
     dma = pltpu.SemaphoreType.DMA
     cache = jax.ShapeDtypeStruct((ROWS, SLOTS, HEAD), BF16)
     part, k_all, v_all = pl.pallas_call(
         attn_kernel,
         out_shape=(jax.ShapeDtypeStruct((NCH, ROWS, CHUNK), BF16), cache, cache),
-        in_specs=[sm] + [vm] * 8 + [hb] * 6,
+        in_specs=[sm] + [hb] * 13,
         out_specs=(vm, hb, hb),
         scratch_shapes=[
+            pltpu.VMEM((1, ROWS), jnp.int32), pltpu.VMEM((1, HEAD), F32), pltpu.VMEM((ROWS, WIDTH), BF16), pltpu.VMEM((WIDTH,), BF16),
+            pltpu.VMEM((4 * HEAD,), BF16), pltpu.VMEM((HEAD,), BF16), pltpu.VMEM((HEAD,), BF16),
             pltpu.VMEM((ROWS, SLOTS, HEAD), BF16), pltpu.VMEM((ROWS, SLOTS, HEAD), BF16),
             pltpu.VMEM((WIDTH, 512), BF16), pltpu.VMEM((WIDTH, HEAD), BF16), pltpu.VMEM((WIDTH, HEAD), BF16), pltpu.VMEM((512, WIDTH), BF16),
             pltpu.VMEM((4, ROWS, HEAD), F32), pltpu.VMEM((ROWS, HEAD), F32), pltpu.VMEM((ROWS, HEAD), F32),
             pltpu.VMEM((128, HEAD), F32), pltpu.VMEM((HEAD, 128), BF16), pltpu.VMEM((SLOTS, 128), F32), pltpu.VMEM((128, SLOTS), BF16),
-            pltpu.VMEM((128, HEAD), F32), pltpu.VMEM((ROWS, 512), BF16),
-            dma((4,)), dma((4,)), dma((4,)), dma((4,)), dma((4,)),
+            pltpu.VMEM((128, HEAD), F32), pltpu.VMEM((ROWS, 512), BF16), pltpu.VMEM((8, 128), jnp.int32),
+            dma((4,)), dma((4,)), dma((4,)), dma((4,)), dma((4,)), dma((7,)),
         ],
         compiler_params=pltpu.CompilerParams(vmem_limit_bytes=VMEM_BYTES),
         name="attention",
-    )(seq_lens, tok_hidden, g_attn.reshape(1, WIDTH), cos_full, sin_full, lane_len, b_q.reshape(1, 512), b_k.reshape(1, HEAD), b_v.reshape(1, HEAD),
+    )(seq_lens, seq_lens.reshape(1, ROWS), freq, tok_hidden, g_attn, b_q, b_k, b_v,
       w_q, w_k, w_v, w_o, k_cache.reshape(ROWS, SLOTS, HEAD), v_cache.reshape(ROWS, SLOTS, HEAD))
 
     ff = w_gate.shape[1]
@@ -437,18 +468,27 @@
     y_out, logp, lse = pl.pallas_call(
         kernel,
         out_shape=(jax.ShapeDtypeStruct((ROWS, WIDTH), BF16), jax.ShapeDtypeStruct((1, ROWS), F32), jax.ShapeDtypeStruct((1, ROWS), F32)),
-        in_specs=[vm] * 5 + [hb] * 4,
+        in_specs=[hb] * 9,
         out_specs=(vm, vm, vm),
         scratch_shapes=[
+            chunk8, pltpu.VMEM((ROWS, WIDTH), BF16), pltpu.VMEM((WIDTH,), BF16), pltpu.VMEM((WIDTH,), BF16), pltpu.VMEM((1, ROWS), jnp.int32),
             pltpu.VMEM((RING, TILE, WIDTH), BF16),
             chunk4, chunk4, chunk4, chunk8, pltpu.VMEM((ROWS, WIDTH), BF16), pltpu.VMEM((ROWS, ff_pad), BF16),
             chunk8, chunk4, chunk4, chunk4, pltpu.VMEM((2, NCH, ROWS, CHUNK), BF16), pltpu.VMEM((2 * ROWS, WIDTH), BF16),
             pltpu.VMEM((1, ROWS), jnp.int32), pltpu.VMEM((2, 8, ROWS), F32), pltpu.VMEM((8, 8, ROWS), F32),
             dma((RING,)),
-        ] + [dma((HALF,))] * 16 + [dma, dma, dma((7,)), dma((7,))],
+        ] + [dma((HALF,))] * 16 + [dma, dma, dma((7,)), dma((7,)), dma((5,))],
         compiler_params=pltpu.CompilerParams(vmem_limit_bytes=VMEM_BYTES, collective_id=0, has_side_effects=True),
         name="tail",
-    )(part, tok_hidden, g_mlp.reshape(1, WIDTH), g_final.reshape(1, WIDTH), next_tok.reshape(1, ROWS), w_gate.T, w_up.T, w_down, w_head)
+    )(part, tok_hidden, g_mlp, g_final, next_tok.reshape(1, ROWS), w_gate.T, w_up.T, w_down, w_head)
+    vec = jax.ShapeDtypeStruct((1, ROWS), F32)
+    y_out, logp, lse = pl.pallas_call(
+        emit_kernel,
+        out_shape=(jax.ShapeDtypeStruct((ROWS, WIDTH), BF16), vec, vec),
+        in_specs=[vm] * 3,
+        out_specs=(vm, vm, vm),
+        name="emit",
+    )(y_out, logp, lse)
     shape = (ROWS, SLOTS, 1, HEAD)
     return y_out, k_all.reshape(shape), v_all.reshape(shape), logp.reshape(ROWS), lse.reshape(ROWS)
 

time: 113 us -> 114 us (level)
  Pallas kernels: 99.9 us -> 113 us
  local copies, waits for them, and re-layouts: 10.8 us -> 0 us
  other arithmetic: 1.73 us -> 0 us
    pallas_call x1, Pallas kernels: 70.2 us -> 84.9 us  [local_step(): pl.pallas_call(kernel, out_shape=(jax.ShapeDtypeStruct((ROWS, WIDTH), BF1...]
    reshape x4 -> x0, local copies, waits for them, and re-layouts: 5.1 us -> none  [the longest x1 1.29 us: local_step(): g_mlp.reshape(1, WIDTH)]
    unnamed x3 -> x0, local copies, waits for them, and re-layouts: 4.16 us -> none
    pallas_call x1, Pallas kernels: 29.6 us -> 26.2 us  [local_step(): pl.pallas_call(attn_kernel, out_shape=(jax.ShapeDtypeStruct((NCH, ROWS, C...]
    pallas_call x0 -> x1, Pallas kernels: none -> 1.88 us  [local_step(): pl.pallas_call(emit_kernel, out_shape=(jax.ShapeDtypeStruct((ROWS, WIDTH)...]
    broadcast_in_dim x3 -> x0, local copies, waits for them, and re-layouts: 1.49 us -> none  [local_step(): lane_len = jnp.repeat(seq_lens, 4).reshape(ROWS // GROUP, 128)]
where the time goes in v2:
time: 114 us
  Pallas kernels  113 us (99%)
    pallas_call x1, Pallas kernels, local_step(): pl.pallas_call(kernel, out_shape=(jax.ShapeDtypeStruct((ROWS, WIDTH), BF1...  84.9 us
    pallas_call x1, Pallas kernels, local_step(): pl.pallas_call(attn_kernel, out_shape=(jax.ShapeDtypeStruct((NCH, ROWS, C...  26.2 us

profile of v2, /device:TPU:0, one launch (start us, length us, event | category | flops | bytes accessed | tf_op | source)
XLA Modules:
  0.0 113.6 jit_solution(18203723890167324429)
XLA Ops:
  0.6 26.2 %attention.1 = (bf16[8,128,256]{2,1,0:T(8,128)(2,1)}, bf16[128,512,128]{2,1,0:T(8,128)(2,1)}, bf16[128,512,128]{2,1,0:T(8,128)(2,1)}) custom-call(s32[128]{0:T(128)} %lens_ref.1, s32[1,128]{1,0:T(1,128)} %bitcast.18, f32[1,128]{1,0:T(1,128)} %constant.2.clone.freq_hbm, bf16[128,2048]{1,0:T(8,128)(2,1)} %refs_1_.1, bf16[2048]{0:T(1024)(128)(2,1)} %g_hbm.1, ...), custom_call_target="tpu_custom_call" | custom-call | tf_op jit(solution)/shard_map/attention/pallas_call | solution.py:439
  26.8 84.9 %tail.1 = (bf16[128,2048]{1,0:T(8,128)(2,1)}, f32[1,128]{1,0:T(1,128)}, f32[1,128]{1,0:T(1,128)}) custom-call(bf16[8,128,256]{2,1,0:T(8,128)(2,1)} %get-tuple-element.14.refs_0_, bf16[128,2048]{1,0:T(8,128)(2,1)} %refs_1_.1, bf16[2048]{0:T(1024)(128)(2,1)} %refs_2_.1, bf16[2048]{0:T(1024)(128)(2,1)} %refs_3_.1, s32[1,128]{1,0:T(1,128)} %bitcast.19, ...), custom_call_target="tpu_custom_call" | custom-call | tf_op jit(solution)/shard_map/tail/pallas_call | solution.py:468
  111.7 1.9 %emit.1 = (bf16[128,2048]{1,0:T(8,128)(2,1)}, f32[1,128]{1,0:T(1,128)}, f32[1,128]{1,0:T(1,128)}) custom-call(bf16[128,2048]{1,0:T(8,128)(2,1)} %get-tuple-element.15.y_in, f32[1,128]{1,0:T(1,128)} %get-tuple-element.16.logp_in, f32[1,128]{1,0:T(1,128)} %get-tuple-element.17.lse_in), custom_call_target="tpu_custom_call" | custom-call | tf_op jit(solution)/shard_map/emit/pallas_call | solution.py:485

commit v3 on v2

--- a/solution.py
+++ b/solution.py
@@ -23,6 +23,7 @@
 HALF = 4
 TILE = 768
 RING = 18
+STEP = 4
 
 
 def dot(a, b):
@@ -53,14 +54,10 @@
             rows = pl.ds(g * GROUP + i * part, part)
             pltpu.make_async_copy(hbm.at[rows], buf.at[rows], sem.at[g]).start()
 
-    for g in range(groups):
-        start_in(g, k_hbm, kbuf, ksem)
-        start_in(g, v_hbm, vbuf, vsem)
-        if g == 0:
-            pltpu.make_async_copy(wo_hbm, wo, wsem.at[3]).start()
-
+    start_in(0, k_hbm, kbuf, ksem)
     for c in small:
         c.wait()
+    start_in(0, v_hbm, vbuf, vsem)
     len_rows = jnp.broadcast_to(lenv_ref[...].astype(F32), (ROWS, ROWS)).T
     angles = len_rows * freq_ref[...]
     cos = jnp.cos(angles)
@@ -76,6 +73,8 @@
     for i, (src, dst) in enumerate(((wq_hbm, wq), (wk_hbm, wk), (wv_hbm, wv))):
         pltpu.make_async_copy(src, dst, wsem.at[i]).wait()
 
+    start_in(1, k_hbm, kbuf, ksem)
+
     def rope(u):
         return u * cos + pltpu.roll(u, HEAD // 2, 1) * sin
 
@@ -93,6 +92,14 @@
     def one_group(g, _):
         rows = pl.ds(pl.multiple_of(g * GROUP, GROUP), GROUP)
         pltpu.make_async_copy(k_hbm.at[rows], kbuf.at[rows], ksem.at[g]).wait()
+
+        @pl.when(g + 1 < groups)
+        def _():
+            start_in(g + 1, v_hbm, vbuf, vsem)
+
+        @pl.when(g + 1 == groups)
+        def _():
+            pltpu.make_async_copy(wo_hbm, wo, wsem.at[3]).start()
 
         def put(new_s, buf):
             def one(i, _):
@@ -103,9 +110,10 @@
                 new = jnp.broadcast_to(new_s[pl.ds(b, 1), :].astype(BF16), (16, HEAD))
                 buf[b, pl.ds(base, 16), :] = jnp.where(row16 == length - base, new, old)
                 return 0
-            lax.fori_loop(0, GROUP, one, 0, unroll=4)
+            lax.fori_loop(0, GROUP, one, 0, unroll=8)
 
         put(k_s, kbuf)
+        pltpu.make_async_copy(kbuf.at[rows], ko_hbm.at[rows], kosem.at[g]).start()
         for h in range(4):
             qg_s[pl.ds(h, GROUP, stride=4), :] = q_s[h, rows, :]
         qt_s[...] = qg_s[...].T.astype(BF16)
@@ -121,7 +129,6 @@
             low_half = t1 if low_half is None else low_half + t1
         sc_s[:SLOTS // 2] = top_half
         sc_s[SLOTS // 2:] = low_half
-        pltpu.make_async_copy(kbuf.at[rows], ko_hbm.at[rows], kosem.at[g]).start()
         live = slot_id <= ll_s[pl.ds(g, 1), :]
         scores = jnp.where(live, sc_s[...] * (HEAD ** -0.5), -jnp.inf)
         top = jnp.max(scores, axis=0, keepdims=True)
@@ -133,7 +140,13 @@
             pt_s[:, i * 128:(i + 1) * 128] = blk.T.astype(BF16)
 
         pltpu.make_async_copy(v_hbm.at[rows], vbuf.at[rows], vsem.at[g]).wait()
+
+        @pl.when(g + 2 < groups)
+        def _():
+            start_in(g + 2, k_hbm, kbuf, ksem)
+
         put(v_s, vbuf)
+        pltpu.make_async_copy(vbuf.at[rows], vo_hbm.at[rows], vosem.at[g]).start()
         for j in range(GROUP // 4):
             b = g * GROUP + 4 * j
             probs = pt_s[16 * j:16 * j + 16, :]
@@ -143,7 +156,6 @@
                 o = jnp.where(row_seq == i, out[:, :HEAD], o)
                 o = jnp.where(row_seq == i + 1, out[:, HEAD:], o)
             o_s[16 * j:16 * j + 16, :] = o
-        pltpu.make_async_copy(vbuf.at[rows], vo_hbm.at[rows], vosem.at[g]).start()
         for h in range(4):
             at_s[rows, h * HEAD:(h + 1) * HEAD] = o_s[pl.ds(h, GROUP, stride=4), :].astype(BF16)
         return 0
@@ -165,7 +177,7 @@
                 y_ref, logp_ref, lse_ref,
                 part_ref, x_ref, gm_ref, gf_ref, tok_ref, wbuf, r1, s1, r2, a_s, m_s, hid, p2, r1b, s2, r2b, y_s, f_s, tok2, st_s, st_r,
                 wsem, s_d1, r_d1, s_x1, r_x1, s_a, r_a, s_d2, r_d2, s_x2, r_x2,
-                s_y, r_y, s_o, r_o, s_f, r_f, s_t, r_t, s_st, r_st, insem):
+                s_y, r_y, s_o, r_o, s_f, r_f, s_t, r_t, s_st, r_st, insem, ysem):
     dp = lax.axis_index('dp')
     tp = lax.axis_index('tp')
     core = lax.rem(tp, 2)
@@ -183,6 +195,7 @@
     n_full = vocab_half // TILE
     n_tail = vocab_half - n_full * TILE
     n_head = n_full + (1 if n_tail else 0)
+    assert n_full % STEP == 0 and n_tail
     head0 = 3 * n_mlp
     vbase = dp * vocab_half
 
@@ -211,8 +224,15 @@
         (part_hbm, part_ref), (x_hbm, x_ref), (gm_hbm, gm_ref), (gf_hbm, gf_ref), (tok_hbm, tok_ref)))]
     for c in small:
         c.start()
-    for i in range(RING):
-        start_item(i)
+    issued = [0]
+
+    def issue(n, freed=0):
+        for _ in range(n):
+            if issued[0] < RING + freed:
+                start_item(issued[0])
+                issued[0] += 1
+
+    issue(2)
 
     barrier = pltpu.get_barrier_semaphore()
     for d in range(2):
@@ -227,6 +247,7 @@
     for c in small:
         c.wait()
     pl.semaphore_wait(barrier, 7)
+    issue(2)
 
     def remote(src, dst, ssem, rsem, who):
         return pltpu.make_async_remote_copy(src_ref=src, dst_ref=dst, send_sem=ssem, recv_sem=rsem, device_id=who, device_id_type=MESH)
@@ -251,13 +272,16 @@
         d1[j].wait_recv()
         s1[j] = (part_ref[mine + j].astype(F32) + r1[j].astype(F32)).astype(BF16)
         x1[j].start()
+    issue(2)
     for j in range(HALF):
         x1[j].wait_recv()
+        issue(2 if j % 2 == 0 else 1)
         total = s1[j].astype(F32) + r2[j].astype(F32)
         a_s[mine + j] = (x_ref[:, cols_of(mine + j)].astype(F32) + total).astype(BF16)
         ac[j].start()
     for j in range(HALF):
         ac[j].wait_recv()
+    issue(1)
 
     def inv_rms(src):
         total = jnp.zeros((ROWS, CHUNK), F32)
@@ -281,8 +305,7 @@
             gate = dot_t(m_s[...], wbuf[gslot, b:b + CHUNK, :])
             up = dot_t(m_s[...], wbuf[uslot, b:b + CHUNK, :])
             hid[:, r + b:r + b + CHUNK] = (gate * jax.nn.sigmoid(gate) * up).astype(BF16)
-        start_item(2 * i + RING)
-        start_item(2 * i + 1 + RING)
+            issue(1, 2 * i)
 
     for i in range(n_mlp):
         mlp_copy(2 * n_mlp + i).wait()
@@ -305,11 +328,11 @@
         p2[other + j] = theirs
         p2[mine + j] = ours
         d2[j].start()
+        issue(1, 2 * n_mlp)
         if j:
             chip_sum(j - 1)
     chip_sum(HALF - 1)
-    for i in range(n_mlp):
-        start_item(2 * n_mlp + i + RING)
+    issue(1, 3 * n_mlp)
 
     def forward(j):
         yy[j].wait_recv()
@@ -317,6 +340,7 @@
 
     for j in range(HALF):
         x2[j].wait_recv()
+        issue(2, 3 * n_mlp)
         total = s2[j].astype(F32) + r2b[j].astype(F32)
         y_s[0, mine + j] = (a_s[mine + j].astype(F32) + total).astype(BF16)
         yy[j].start()
@@ -326,8 +350,10 @@
     forward(HALF - 1)
     for j in range(HALF):
         yo[j].wait_recv()
-    for c in range(NCH):
-        y_ref[:, c * CHUNK:(c + 1) * CHUNK] = y_s[0, c]
+    issue(RING, 3 * n_mlp)
+    y_out = [pltpu.make_async_copy(y_s.at[0, c], y_ref.at[:, pl.ds(c * CHUNK, CHUNK)], ysem.at[c]) for c in range(NCH)]
+    for c in y_out:
+        c.start()
 
     gf = gf_ref[...].astype(F32).reshape(1, WIDTH)
 
@@ -346,44 +372,47 @@
     tok = jnp.concatenate([tok_ref[...], tok2[...]], axis=1) - (tp * vocab_loc + vbase)
     row_id = lax.broadcasted_iota(jnp.int32, (8, 2 * ROWS), 0)
 
-    def score(slot, first, n, state):
+    def score(slot, at, size, first, state):
         top, tot, tgt = state
-        cut = -(-n // 32) * 16
-        for b, size in ((0, cut), (cut, n - cut)):
-            logits = dot_t(wbuf[slot, pl.ds(b, size), :], f_s[...])
-            blocks = [logits[8 * i:8 * i + 8] for i in range(size // 8)]
-            peak = blocks[0]
-            for v in blocks[1:]:
-                peak = jnp.maximum(peak, v)
-            new = jnp.maximum(top, peak)
-            part_sum = None
-            for i, v in enumerate(blocks):
-                e = jnp.exp(v - new)
-                part_sum = e if part_sum is None else part_sum + e
-                tgt = jnp.where(row_id + (first + b + 8 * i) == tok, v, tgt)
-            tot = tot * jnp.exp(top - new) + part_sum
-            top = new
-        return top, tot, tgt
-
-    def one_tile(i, state):
-        slot = lax.rem(head0 + i, RING)
-        head_copy(i).wait()
-        state = score(slot, i * TILE, TILE, state)
-
-        @pl.when(i + RING < n_full)
-        def _():
-            head_copy(i + RING).start()
-        if n_tail:
-            @pl.when(i + RING == n_full)
+        logits = dot_t(wbuf[slot, pl.ds(at, size), :], f_s[...])
+        blocks = [logits[8 * i:8 * i + 8] for i in range(size // 8)]
+        peak = blocks[0]
+        for v in blocks[1:]:
+            peak = jnp.maximum(peak, v)
+        new = jnp.maximum(top, peak)
+        part_sum = None
+        for i, v in enumerate(blocks):
+            e = jnp.exp(v - new)
+            part_sum = e if part_sum is None else part_sum + e
+            tgt = jnp.where(row_id + (first + 8 * i) == tok, v, tgt)
+        tot = tot * jnp.exp(top - new) + part_sum
+        return new, tot, tgt
+
+    def some_tiles(k, state):
+        for t in range(STEP):
+            head_copy(k * STEP + t).wait()
+        for t in range(STEP):
+            i = k * STEP + t
+            for b in range(0, TILE, CHUNK):
+                state = score(lax.rem(head0 + i, RING), b, CHUNK, i * TILE + b, state)
+        for t in range(STEP):
+            i = k * STEP + t
+
+            @pl.when(i + RING < n_full)
             def _():
-                head_copy(n_full, n_tail).start()
+                head_copy(i + RING).start()
+            if n_tail:
+                @pl.when(i + RING == n_full)
+                def _():
+                    head_copy(n_full, n_tail).start()
         return state
 
     state = (jnp.full((8, 2 * ROWS), -1e30, F32), jnp.zeros((8, 2 * ROWS), F32), jnp.zeros((8, 2 * ROWS), F32))
-    state = lax.fori_loop(0, n_full, one_tile, state)
-    if n_tail:
-        head_copy(n_full, n_tail).wait()
-        state = score((head0 + n_full) % RING, n_full * TILE, n_tail, state)
+    state = lax.fori_loop(0, n_full // STEP, some_tiles, state)
+    head_copy(n_full, n_tail).wait()
+    cut = -(-n_tail // 32) * 16
+    for b, size in ((0, cut), (cut, n_tail - cut)):
+        state = score((head0 + n_full) % RING, b, size, n_full * TILE + b, state)
     top, tot, tgt = state
     peak = jnp.max(top, axis=0, keepdims=True)
     tot = jnp.sum(tot * jnp.exp(top - peak), axis=0, keepdims=True)
@@ -420,6 +449,8 @@
     for group in (d1, x1, ac, d2, x2, yo, yy, yf):
         for c in group:
             c.wait_send()
+    for c in y_out:
+        c.wait()
 
 
 def emit_kernel(y_in, logp_in, lse_in, y_out, logp_out, lse_out):
@@ -469,7 +500,7 @@
         kernel,
         out_shape=(jax.ShapeDtypeStruct((ROWS, WIDTH), BF16), jax.ShapeDtypeStruct((1, ROWS), F32), jax.ShapeDtypeStruct((1, ROWS), F32)),
         in_specs=[hb] * 9,
-        out_specs=(vm, vm, vm),
+        out_specs=(hb, vm, vm),
         scratch_shapes=[
             chunk8, pltpu.VMEM((ROWS, WIDTH), BF16), pltpu.VMEM((WIDTH,), BF16), pltpu.VMEM((WIDTH,), BF16), pltpu.VMEM((1, ROWS), jnp.int32),
             pltpu.VMEM((RING, TILE, WIDTH), BF16),
@@ -477,7 +508,7 @@
             chunk8, chunk4, chunk4, chunk4, pltpu.VMEM((2, NCH, ROWS, CHUNK), BF16), pltpu.VMEM((2 * ROWS, WIDTH), BF16),
             pltpu.VMEM((1, ROWS), jnp.int32), pltpu.VMEM((2, 8, ROWS), F32), pltpu.VMEM((8, 8, ROWS), F32),
             dma((RING,)),
-        ] + [dma((HALF,))] * 16 + [dma, dma, dma((7,)), dma((7,)), dma((5,))],
+        ] + [dma((HALF,))] * 16 + [dma, dma, dma((7,)), dma((7,)), dma((5,)), dma((NCH,))],
         compiler_params=pltpu.CompilerParams(vmem_limit_bytes=VMEM_BYTES, collective_id=0, has_side_effects=True),
         name="tail",
     )(part, tok_hidden, g_mlp, g_final, next_tok.reshape(1, ROWS), w_gate.T, w_up.T, w_down, w_head)

time: 114 us -> 96.6 us (0.85)
  Pallas kernels: 113 us -> 95.8 us
    pallas_call x1, Pallas kernels: 84.9 us -> 67.8 us  [local_step(): pl.pallas_call(kernel, out_shape=(jax.ShapeDtypeStruct((ROWS, WIDTH), BF1...]
where the time goes in v3:
time: 96.6 us; the launch traced here: 96.5 us
  Pallas kernels  95.8 us (99%)
    pallas_call x1, Pallas kernels, local_step(): pl.pallas_call(kernel, out_shape=(jax.ShapeDtypeStruct((ROWS, WIDTH), BF1...  67.8 us
    pallas_call x1, Pallas kernels, local_step(): pl.pallas_call(attn_kernel, out_shape=(jax.ShapeDtypeStruct((NCH, ROWS, C...  26.1 us

profile of v3, /device:TPU:0, one launch (start us, length us, event | category | flops | bytes accessed | tf_op | source)
XLA Modules:
  0.0 96.5 jit_solution(5827206781034479749)
XLA Ops:
  0.6 26.1 %attention.1 = (bf16[8,128,256]{2,1,0:T(8,128)(2,1)}, bf16[128,512,128]{2,1,0:T(8,128)(2,1)}, bf16[128,512,128]{2,1,0:T(8,128)(2,1)}) custom-call(s32[128]{0:T(128)} %lens_ref.1, s32[1,128]{1,0:T(1,128)} %bitcast.18, f32[1,128]{1,0:T(1,128)} %constant.2.clone.freq_hbm, bf16[128,2048]{1,0:T(8,128)(2,1)} %refs_1_.1, bf16[2048]{0:T(1024)(128)(2,1)} %g_hbm.1, ...), custom_call_target="tpu_custom_call" | custom-call | tf_op jit(solution)/shard_map/attention/pallas_call | solution.py:470
  26.8 67.8 %tail.1 = (bf16[128,2048]{1,0:T(8,128)(2,1)}, f32[1,128]{1,0:T(1,128)}, f32[1,128]{1,0:T(1,128)}) custom-call(bf16[8,128,256]{2,1,0:T(8,128)(2,1)} %get-tuple-element.14.refs_0_, bf16[128,2048]{1,0:T(8,128)(2,1)} %refs_1_.1, bf16[2048]{0:T(1024)(128)(2,1)} %refs_2_.1, bf16[2048]{0:T(1024)(128)(2,1)} %refs_3_.1, s32[1,128]{1,0:T(1,128)} %bitcast.19, ...), custom_call_target="tpu_custom_call" | custom-call | tf_op jit(solution)/shard_map/tail/pallas_call | solution.py:499
  94.6 1.9 %emit.1 = (bf16[128,2048]{1,0:T(8,128)(2,1)}, f32[1,128]{1,0:T(1,128)}, f32[1,128]{1,0:T(1,128)}) custom-call(bf16[128,2048]{1,0:T(8,128)(2,1)} %get-tuple-element.15.y_in, f32[1,128]{1,0:T(1,128)} %get-tuple-element.16.logp_in, f32[1,128]{1,0:T(1,128)} %get-tuple-element.17.lse_in), custom_call_target="tpu_custom_call" | custom-call | tf_op jit(solution)/shard_map/emit/pallas_call | solution.py:516

commit v4 on v3

--- a/solution.py
+++ b/solution.py
@@ -18,9 +18,10 @@
 HEAD = 128
 SLOTS = 512
 GROUP = 32
-CHUNK = 256
-NCH = 8
-HALF = 4
+CHUNK = 128
+NCH = 16
+HALF = 8
+BLOCK = 256
 TILE = 768
 RING = 18
 STEP = 4
@@ -36,8 +37,8 @@
 
 def attn_kernel(lens_ref, lenv_hbm, freq_hbm, x_hbm, g_hbm, bq_hbm, bk_hbm, bv_hbm,
                 wq_hbm, wk_hbm, wv_hbm, wo_hbm, k_hbm, v_hbm,
-                part_ref, ko_hbm, vo_hbm,
-                lenv_ref, freq_ref, x_ref, g_ref, bq_ref, bk_ref, bv_ref,
+                part_hbm, ko_hbm, vo_hbm,
+                part_ref, lenv_ref, freq_ref, x_ref, g_ref, bq_ref, bk_ref, bv_ref,
                 kbuf, vbuf, wq, wk, wv, wo, q_s, k_s, v_s, qg_s, qt_s, sc_s, pt_s, o_s, at_s, ll_s,
                 wsem, ksem, vsem, kosem, vosem, insem):
     groups = ROWS // GROUP
@@ -89,6 +90,11 @@
     row16 = lax.broadcasted_iota(jnp.int32, (16, HEAD), 0)
     row_seq = lax.broadcasted_iota(jnp.int32, (16, HEAD), 0) // 4
 
+    def start_out(g):
+        rows = pl.ds(g * GROUP, GROUP)
+        pltpu.make_async_copy(kbuf.at[rows], ko_hbm.at[rows], kosem.at[g]).start()
+        pltpu.make_async_copy(vbuf.at[rows], vo_hbm.at[rows], vosem.at[g]).start()
+
     def one_group(g, _):
         rows = pl.ds(pl.multiple_of(g * GROUP, GROUP), GROUP)
         pltpu.make_async_copy(k_hbm.at[rows], kbuf.at[rows], ksem.at[g]).wait()
@@ -113,7 +119,13 @@
             lax.fori_loop(0, GROUP, one, 0, unroll=8)
 
         put(k_s, kbuf)
-        pltpu.make_async_copy(kbuf.at[rows], ko_hbm.at[rows], kosem.at[g]).start()
+
+        @pl.when(g + 1 == groups)
+        def _():
+            for i in range(groups - 1):
+                start_out(i)
+            pltpu.make_async_copy(kbuf.at[rows], ko_hbm.at[rows], kosem.at[g]).start()
+
         for h in range(4):
             qg_s[pl.ds(h, GROUP, stride=4), :] = q_s[h, rows, :]
         qt_s[...] = qg_s[...].T.astype(BF16)
@@ -146,7 +158,11 @@
             start_in(g + 2, k_hbm, kbuf, ksem)
 
         put(v_s, vbuf)
-        pltpu.make_async_copy(vbuf.at[rows], vo_hbm.at[rows], vosem.at[g]).start()
+
+        @pl.when(g + 1 == groups)
+        def _():
+            pltpu.make_async_copy(vbuf.at[rows], vo_hbm.at[rows], vosem.at[g]).start()
+
         for j in range(GROUP // 4):
             b = g * GROUP + 4 * j
             probs = pt_s[16 * j:16 * j + 16, :]
@@ -164,8 +180,13 @@
 
     pltpu.make_async_copy(wo_hbm, wo, wsem.at[3]).wait()
     attn = at_s[...]
-    for c in range(NCH):
-        part_ref[c] = dot(attn, wo[:, c * CHUNK:(c + 1) * CHUNK]).astype(BF16)
+    for c in range(WIDTH // BLOCK):
+        block = dot(attn, wo[:, c * BLOCK:(c + 1) * BLOCK]).astype(BF16)
+        part_ref[2 * c] = block[:, :CHUNK]
+        part_ref[2 * c + 1] = block[:, CHUNK:]
+    part_copy = pltpu.make_async_copy(part_ref, part_hbm, insem.at[7])
+    part_copy.start()
+    part_copy.wait()
     for g in range(groups):
         rows = pl.ds(g * GROUP, GROUP)
         pltpu.make_async_copy(kbuf.at[rows], ko_hbm.at[rows], kosem.at[g]).wait()
@@ -190,7 +211,7 @@
 
     mlp_tiles = [(i * TILE, min(TILE, ff - i * TILE)) for i in range(-(-ff // TILE))]
     n_mlp = len(mlp_tiles)
-    tail_pad = -(-mlp_tiles[-1][1] // CHUNK) * CHUNK
+    tail_pad = -(-mlp_tiles[-1][1] // BLOCK) * BLOCK
     vocab_half = vocab_loc // 2
     n_full = vocab_half // TILE
     n_tail = vocab_half - n_full * TILE
@@ -275,7 +296,7 @@
     issue(2)
     for j in range(HALF):
         x1[j].wait_recv()
-        issue(2 if j % 2 == 0 else 1)
+        issue(1 if j % 4 < 3 else 0)
         total = s1[j].astype(F32) + r2[j].astype(F32)
         a_s[mine + j] = (x_ref[:, cols_of(mine + j)].astype(F32) + total).astype(BF16)
         ac[j].start()
@@ -300,21 +321,22 @@
         mlp_copy(2 * i).wait()
         mlp_copy(2 * i + 1).wait()
         gslot, uslot = (2 * i) % RING, (2 * i + 1) % RING
-        pad = -(-n // CHUNK) * CHUNK
-        for b in range(0, pad, CHUNK):
-            gate = dot_t(m_s[...], wbuf[gslot, b:b + CHUNK, :])
-            up = dot_t(m_s[...], wbuf[uslot, b:b + CHUNK, :])
-            hid[:, r + b:r + b + CHUNK] = (gate * jax.nn.sigmoid(gate) * up).astype(BF16)
+        pad = -(-n // BLOCK) * BLOCK
+        for b in range(0, pad, BLOCK):
+            gate = dot_t(m_s[...], wbuf[gslot, b:b + BLOCK, :])
+            up = dot_t(m_s[...], wbuf[uslot, b:b + BLOCK, :])
+            hid[:, r + b:r + b + BLOCK] = (gate * jax.nn.sigmoid(gate) * up).astype(BF16)
             issue(1, 2 * i)
 
     for i in range(n_mlp):
         mlp_copy(2 * n_mlp + i).wait()
 
-    def down(c):
+    def down(base, j):
+        cols = pl.ds(pl.multiple_of((base + 2 * j) * CHUNK, BLOCK), BLOCK)
         acc = None
         for i, (r, n) in enumerate(mlp_tiles):
-            pad = -(-n // CHUNK) * CHUNK
-            term = dot(hid[:, r:r + pad], wbuf[(2 * n_mlp + i) % RING, :pad, cols_of(c)])
+            pad = -(-n // BLOCK) * BLOCK
+            term = dot(hid[:, r:r + pad], wbuf[(2 * n_mlp + i) % RING, :pad, cols])
             acc = term if acc is None else acc + term
         return acc.astype(BF16)
 
@@ -323,14 +345,19 @@
         s2[j] = (p2[mine + j].astype(F32) + r1b[j].astype(F32)).astype(BF16)
         x2[j].start()
 
-    for j in range(HALF):
-        theirs, ours = down(other + j), down(mine + j)
-        p2[other + j] = theirs
-        p2[mine + j] = ours
-        d2[j].start()
+    for j in range(HALF // 2):
+        theirs, ours = down(other, j), down(mine, j)
+        for i in range(2):
+            cols = slice(i * CHUNK, (i + 1) * CHUNK)
+            p2[other + 2 * j + i] = theirs[:, cols]
+            p2[mine + 2 * j + i] = ours[:, cols]
+        for i in range(2):
+            d2[2 * j + i].start()
         issue(1, 2 * n_mlp)
         if j:
-            chip_sum(j - 1)
+            chip_sum(2 * j - 2)
+            chip_sum(2 * j - 1)
+    chip_sum(HALF - 2)
     chip_sum(HALF - 1)
     issue(1, 3 * n_mlp)
 
@@ -340,7 +367,7 @@
 
     for j in range(HALF):
         x2[j].wait_recv()
-        issue(2, 3 * n_mlp)
+        issue(1, 3 * n_mlp)
         total = s2[j].astype(F32) + r2b[j].astype(F32)
         y_s[0, mine + j] = (a_s[mine + j].astype(F32) + total).astype(BF16)
         yy[j].start()
@@ -393,8 +420,8 @@
             head_copy(k * STEP + t).wait()
         for t in range(STEP):
             i = k * STEP + t
-            for b in range(0, TILE, CHUNK):
-                state = score(lax.rem(head0 + i, RING), b, CHUNK, i * TILE + b, state)
+            for b in range(0, TILE, BLOCK):
+                state = score(lax.rem(head0 + i, RING), b, BLOCK, i * TILE + b, state)
         for t in range(STEP):
             i = k * STEP + t
 
@@ -453,10 +480,15 @@
         c.wait()
 
 
-def emit_kernel(y_in, logp_in, lse_in, y_out, logp_out, lse_out):
-    y_out[...] = y_in[...]
-    logp_out[...] = logp_in[...]
-    lse_out[...] = lse_in[...]
+def emit_kernel(y_in, logp_in, lse_in, y_out, logp_out, lse_out, sem):
+    copies = [pltpu.make_async_copy(logp_in, logp_out, sem.at[0]), pltpu.make_async_copy(lse_in, lse_out, sem.at[1])]
+    for i in range(8):
+        rows = pl.ds(i * 16, 16)
+        copies.append(pltpu.make_async_copy(y_in.at[rows], y_out.at[rows], sem.at[2 + i]))
+    for c in copies:
+        c.start()
+    for c in copies:
+        c.wait()
 
 
 def local_step(tok_hidden, seq_lens, k_cache, v_cache, next_tok, g_attn, w_q, b_q, w_k, b_k, w_v, b_v, w_o, g_mlp, w_gate, w_up, w_down, g_final, w_head):
@@ -471,16 +503,16 @@
         attn_kernel,
         out_shape=(jax.ShapeDtypeStruct((NCH, ROWS, CHUNK), BF16), cache, cache),
         in_specs=[sm] + [hb] * 13,
-        out_specs=(vm, hb, hb),
+        out_specs=(hb, hb, hb),
         scratch_shapes=[
-            pltpu.VMEM((1, ROWS), jnp.int32), pltpu.VMEM((1, HEAD), F32), pltpu.VMEM((ROWS, WIDTH), BF16), pltpu.VMEM((WIDTH,), BF16),
+            pltpu.VMEM((NCH, ROWS, CHUNK), BF16), pltpu.VMEM((1, ROWS), jnp.int32), pltpu.VMEM((1, HEAD), F32), pltpu.VMEM((ROWS, WIDTH), BF16), pltpu.VMEM((WIDTH,), BF16),
             pltpu.VMEM((4 * HEAD,), BF16), pltpu.VMEM((HEAD,), BF16), pltpu.VMEM((HEAD,), BF16),
             pltpu.VMEM((ROWS, SLOTS, HEAD), BF16), pltpu.VMEM((ROWS, SLOTS, HEAD), BF16),
             pltpu.VMEM((WIDTH, 512), BF16), pltpu.VMEM((WIDTH, HEAD), BF16), pltpu.VMEM((WIDTH, HEAD), BF16), pltpu.VMEM((512, WIDTH), BF16),
             pltpu.VMEM((4, ROWS, HEAD), F32), pltpu.VMEM((ROWS, HEAD), F32), pltpu.VMEM((ROWS, HEAD), F32),
             pltpu.VMEM((128, HEAD), F32), pltpu.VMEM((HEAD, 128), BF16), pltpu.VMEM((SLOTS, 128), F32), pltpu.VMEM((128, SLOTS), BF16),
             pltpu.VMEM((128, HEAD), F32), pltpu.VMEM((ROWS, 512), BF16), pltpu.VMEM((8, 128), jnp.int32),
-            dma((4,)), dma((4,)), dma((4,)), dma((4,)), dma((4,)), dma((7,)),
+            dma((4,)), dma((4,)), dma((4,)), dma((4,)), dma((4,)), dma((8,)),
         ],
         compiler_params=pltpu.CompilerParams(vmem_limit_bytes=VMEM_BYTES),
         name="attention",
@@ -489,7 +521,7 @@
 
     ff = w_gate.shape[1]
     vocab_loc = w_head.shape[0]
-    ff_pad = -(-ff // CHUNK) * CHUNK
+    ff_pad = -(-ff // BLOCK) * BLOCK
     chunk4 = pltpu.VMEM((HALF, ROWS, CHUNK), BF16)
     chunk8 = pltpu.VMEM((NCH, ROWS, CHUNK), BF16)
 
@@ -516,8 +548,9 @@
     y_out, logp, lse = pl.pallas_call(
         emit_kernel,
         out_shape=(jax.ShapeDtypeStruct((ROWS, WIDTH), BF16), vec, vec),
-        in_specs=[vm] * 3,
-        out_specs=(vm, vm, vm),
+        in_specs=[hb] * 3,
+        out_specs=(hb, hb, hb),
+        scratch_shapes=[dma((10,))],
         name="emit",
     )(y_out, logp, lse)
     shape = (ROWS, SLOTS, 1, HEAD)

time: 96.6 us -> 114 us (1.18)
  Pallas kernels: 95.8 us -> 113 us
    pallas_call x1, Pallas kernels: 1.88 us -> 17.1 us  [local_step(): pl.pallas_call(emit_kernel, out_shape=(jax.ShapeDtypeStruct((ROWS, WIDTH)...]
    pallas_call x1, Pallas kernels: 67.8 us -> 71.9 us  [local_step(): pl.pallas_call(kernel, out_shape=(jax.ShapeDtypeStruct((ROWS, WIDTH), BF1...]
    pallas_call x1, Pallas kernels: 26.1 us -> 24.3 us  [local_step(): pl.pallas_call(attn_kernel, out_shape=(jax.ShapeDtypeStruct((NCH, ROWS, C...]
where the time goes in v4:
time: 114 us
  Pallas kernels  113 us (99%)
    pallas_call x1, Pallas kernels, local_step(): pl.pallas_call(kernel, out_shape=(jax.ShapeDtypeStruct((ROWS, WIDTH), BF1...  71.9 us
    pallas_call x1, Pallas kernels, local_step(): pl.pallas_call(attn_kernel, out_shape=(jax.ShapeDtypeStruct((NCH, ROWS, C...  24.3 us
    pallas_call x1, Pallas kernels, local_step(): pl.pallas_call(emit_kernel, out_shape=(jax.ShapeDtypeStruct((ROWS, WIDTH)...  17.1 us

profile of v4, /device:TPU:0, one launch (start us, length us, event | category | flops | bytes accessed | tf_op | source)
XLA Modules:
  0.0 114.1 jit_solution(10653858970965202839)
XLA Ops:
  0.6 24.3 %attention.1 = (bf16[16,128,128]{2,1,0:T(8,128)(2,1)}, bf16[128,512,128]{2,1,0:T(8,128)(2,1)}, bf16[128,512,128]{2,1,0:T(8,128)(2,1)}) custom-call(s32[128]{0:T(128)} %lens_ref.1, s32[1,128]{1,0:T(1,128)} %bitcast.18, f32[1,128]{1,0:T(1,128)} %constant.2.clone.freq_hbm, bf16[128,2048]{1,0:T(8,128)(2,1)} %refs_1_.1, bf16[2048]{0:T(1024)(128)(2,1)} %g_hbm.1, ...), custom_call_target="tpu_custom_call" | custom-call | tf_op jit(solution)/shard_map/attention/pallas_call | solution.py:502
  24.9 71.9 %tail.1 = (bf16[128,2048]{1,0:T(8,128)(2,1)}, f32[1,128]{1,0:T(1,128)}, f32[1,128]{1,0:T(1,128)}) custom-call(bf16[16,128,128]{2,1,0:T(8,128)(2,1)} %get-tuple-element.14.refs_0_, bf16[128,2048]{1,0:T(8,128)(2,1)} %refs_1_.1, bf16[2048]{0:T(1024)(128)(2,1)} %refs_2_.1, bf16[2048]{0:T(1024)(128)(2,1)} %refs_3_.1, s32[1,128]{1,0:T(1,128)} %bitcast.19, ...), custom_call_target="tpu_custom_call" | custom-call | tf_op jit(solution)/shard_map/tail/pallas_call | solution.py:531
  96.9 17.1 %emit.1 = (bf16[128,2048]{1,0:T(8,128)(2,1)}, f32[1,128]{1,0:T(1,128)}, f32[1,128]{1,0:T(1,128)}) custom-call(bf16[128,2048]{1,0:T(8,128)(2,1)} %get-tuple-element.15.y_in, f32[1,128]{1,0:T(1,128)} %get-tuple-element.16.logp_in, f32[1,128]{1,0:T(1,128)} %get-tuple-element.17.lse_in), custom_call_target="tpu_custom_call" | custom-call | tf_op jit(solution)/shard_map/emit/pallas_call | solution.py:548

commit v5 on v4

--- a/solution.py
+++ b/solution.py
@@ -18,10 +18,12 @@
 HEAD = 128
 SLOTS = 512
 GROUP = 32
-CHUNK = 128
-NCH = 16
-HALF = 8
+CHUNK = 256
+NCH = 8
+HALF = 4
 BLOCK = 256
+SUM1 = ((0, 2), (2, 2))
+SUM2 = ((0, 2), (2, 1), (3, 1))
 TILE = 768
 RING = 18
 STEP = 4
@@ -181,9 +183,7 @@
     pltpu.make_async_copy(wo_hbm, wo, wsem.at[3]).wait()
     attn = at_s[...]
     for c in range(WIDTH // BLOCK):
-        block = dot(attn, wo[:, c * BLOCK:(c + 1) * BLOCK]).astype(BF16)
-        part_ref[2 * c] = block[:, :CHUNK]
-        part_ref[2 * c + 1] = block[:, CHUNK:]
+        part_ref[c] = dot(attn, wo[:, c * BLOCK:(c + 1) * BLOCK]).astype(BF16)
     part_copy = pltpu.make_async_copy(part_ref, part_hbm, insem.at[7])
     part_copy.start()
     part_copy.wait()
@@ -274,34 +274,39 @@
         return pltpu.make_async_remote_copy(src_ref=src, dst_ref=dst, send_sem=ssem, recv_sem=rsem, device_id=who, device_id_type=MESH)
 
     tok_copy = remote(tok_ref, tok2, s_t, r_t, ynext)
-    d1 = [remote(part_ref.at[other + j], r1.at[j], s_d1.at[j], r_d1.at[j], partner) for j in range(HALF)]
-    x1 = [remote(s1.at[j], r2.at[j], s_x1.at[j], r_x1.at[j], xnext) for j in range(HALF)]
-    ac = [remote(a_s.at[mine + j], a_s.at[mine + j], s_a.at[j], r_a.at[j], partner) for j in range(HALF)]
-    d2 = [remote(p2.at[other + j], r1b.at[j], s_d2.at[j], r_d2.at[j], partner) for j in range(HALF)]
-    x2 = [remote(s2.at[j], r2b.at[j], s_x2.at[j], r_x2.at[j], xnext) for j in range(HALF)]
-    yo = [remote(y_s.at[0, mine + j], y_s.at[0, mine + j], s_o.at[j], r_o.at[j], partner) for j in range(HALF)]
-    yy = [remote(y_s.at[0, mine + j], y_s.at[1, mine + j], s_y.at[j], r_y.at[j], ynext) for j in range(HALF)]
-    yf = [remote(y_s.at[1, mine + j], y_s.at[1, mine + j], s_f.at[j], r_f.at[j], partner) for j in range(HALF)]
+    def part_of(ref, base, grp):
+        return ref.at[pl.ds(base + grp[0], grp[1])]
+
+    d1 = [remote(part_of(part_ref, other, p), part_of(r1, 0, p), s_d1.at[i], r_d1.at[i], partner) for i, p in enumerate(SUM1)]
+    x1 = [remote(part_of(s1, 0, p), part_of(r2, 0, p), s_x1.at[i], r_x1.at[i], xnext) for i, p in enumerate(SUM1)]
+    ac = [remote(part_of(a_s, mine, p), part_of(a_s, mine, p), s_a.at[i], r_a.at[i], partner) for i, p in enumerate(SUM1)]
+    d2 = [remote(part_of(p2, other, p), part_of(r1b, 0, p), s_d2.at[i], r_d2.at[i], partner) for i, p in enumerate(SUM2)]
+    x2 = [remote(part_of(s2, 0, p), part_of(r2b, 0, p), s_x2.at[i], r_x2.at[i], xnext) for i, p in enumerate(SUM2)]
+    yo = [remote(part_of(y_s.at[0], mine, p), part_of(y_s.at[0], mine, p), s_o.at[i], r_o.at[i], partner) for i, p in enumerate(SUM2)]
+    yy = [remote(part_of(y_s.at[0], mine, p), part_of(y_s.at[1], mine, p), s_y.at[i], r_y.at[i], ynext) for i, p in enumerate(SUM2)]
+    yf = [remote(part_of(y_s.at[1], mine, p), part_of(y_s.at[1], mine, p), s_f.at[i], r_f.at[i], partner) for i, p in enumerate(SUM2)]
 
     def cols_of(c):
         return pl.ds(pl.multiple_of(c * CHUNK, CHUNK), CHUNK)
 
-    for j in range(HALF):
-        d1[j].start()
+    for c in d1:
+        c.start()
     tok_copy.start()
-    for j in range(HALF):
-        d1[j].wait_recv()
-        s1[j] = (part_ref[mine + j].astype(F32) + r1[j].astype(F32)).astype(BF16)
-        x1[j].start()
+    for i, (first, n) in enumerate(SUM1):
+        d1[i].wait_recv()
+        for j in range(first, first + n):
+            s1[j] = (part_ref[mine + j].astype(F32) + r1[j].astype(F32)).astype(BF16)
+        x1[i].start()
     issue(2)
-    for j in range(HALF):
-        x1[j].wait_recv()
-        issue(1 if j % 4 < 3 else 0)
-        total = s1[j].astype(F32) + r2[j].astype(F32)
-        a_s[mine + j] = (x_ref[:, cols_of(mine + j)].astype(F32) + total).astype(BF16)
-        ac[j].start()
-    for j in range(HALF):
-        ac[j].wait_recv()
+    for i, (first, n) in enumerate(SUM1):
+        x1[i].wait_recv()
+        issue(3)
+        for j in range(first, first + n):
+            total = s1[j].astype(F32) + r2[j].astype(F32)
+            a_s[mine + j] = (x_ref[:, cols_of(mine + j)].astype(F32) + total).astype(BF16)
+        ac[i].start()
+    for c in ac:
+        c.wait_recv()
     issue(1)
 
     def inv_rms(src):
@@ -331,52 +336,50 @@
     for i in range(n_mlp):
         mlp_copy(2 * n_mlp + i).wait()
 
-    def down(base, j):
-        cols = pl.ds(pl.multiple_of((base + 2 * j) * CHUNK, BLOCK), BLOCK)
+    def down(c):
         acc = None
         for i, (r, n) in enumerate(mlp_tiles):
             pad = -(-n // BLOCK) * BLOCK
-            term = dot(hid[:, r:r + pad], wbuf[(2 * n_mlp + i) % RING, :pad, cols])
+            term = dot(hid[:, r:r + pad], wbuf[(2 * n_mlp + i) % RING, :pad, cols_of(c)])
             acc = term if acc is None else acc + term
         return acc.astype(BF16)
 
-    def chip_sum(j):
-        d2[j].wait_recv()
-        s2[j] = (p2[mine + j].astype(F32) + r1b[j].astype(F32)).astype(BF16)
-        x2[j].start()
-
-    for j in range(HALF // 2):
-        theirs, ours = down(other, j), down(mine, j)
-        for i in range(2):
-            cols = slice(i * CHUNK, (i + 1) * CHUNK)
-            p2[other + 2 * j + i] = theirs[:, cols]
-            p2[mine + 2 * j + i] = ours[:, cols]
-        for i in range(2):
-            d2[2 * j + i].start()
-        issue(1, 2 * n_mlp)
-        if j:
-            chip_sum(2 * j - 2)
-            chip_sum(2 * j - 1)
-    chip_sum(HALF - 2)
-    chip_sum(HALF - 1)
+    def chip_sum(i):
+        d2[i].wait_recv()
+        first, n = SUM2[i]
+        for j in range(first, first + n):
+            s2[j] = (p2[mine + j].astype(F32) + r1b[j].astype(F32)).astype(BF16)
+        x2[i].start()
+
+    for i, (first, n) in enumerate(SUM2):
+        for j in range(first, first + n):
+            theirs, ours = down(other + j), down(mine + j)
+            p2[other + j] = theirs
+            p2[mine + j] = ours
+            issue(1, 2 * n_mlp)
+        d2[i].start()
+        if i:
+            chip_sum(i - 1)
+    chip_sum(len(SUM2) - 1)
     issue(1, 3 * n_mlp)
 
-    def forward(j):
-        yy[j].wait_recv()
-        yf[j].start()
-
-    for j in range(HALF):
-        x2[j].wait_recv()
-        issue(1, 3 * n_mlp)
-        total = s2[j].astype(F32) + r2b[j].astype(F32)
-        y_s[0, mine + j] = (a_s[mine + j].astype(F32) + total).astype(BF16)
-        yy[j].start()
-        yo[j].start()
-        if j:
-            forward(j - 1)
-    forward(HALF - 1)
-    for j in range(HALF):
-        yo[j].wait_recv()
+    def forward(i):
+        yy[i].wait_recv()
+        yf[i].start()
+
+    for i, (first, n) in enumerate(SUM2):
+        x2[i].wait_recv()
+        issue(2, 3 * n_mlp)
+        for j in range(first, first + n):
+            total = s2[j].astype(F32) + r2b[j].astype(F32)
+            y_s[0, mine + j] = (a_s[mine + j].astype(F32) + total).astype(BF16)
+        yy[i].start()
+        yo[i].start()
+        if i:
+            forward(i - 1)
+    forward(len(SUM2) - 1)
+    for c in yo:
+        c.wait_recv()
     issue(RING, 3 * n_mlp)
     y_out = [pltpu.make_async_copy(y_s.at[0, c], y_ref.at[:, pl.ds(c * CHUNK, CHUNK)], ysem.at[c]) for c in range(NCH)]
     for c in y_out:
@@ -391,8 +394,8 @@
             f_s[grp * ROWS:(grp + 1) * ROWS, cols] = (y_s[grp, c].astype(F32) * inv * gf[:, cols]).astype(BF16)
 
     final_norm(0)
-    for j in range(HALF):
-        yf[j].wait_recv()
+    for c in yf:
+        c.wait_recv()
     final_norm(1)
     tok_copy.wait()
 
@@ -480,15 +483,10 @@
         c.wait()
 
 
-def emit_kernel(y_in, logp_in, lse_in, y_out, logp_out, lse_out, sem):
-    copies = [pltpu.make_async_copy(logp_in, logp_out, sem.at[0]), pltpu.make_async_copy(lse_in, lse_out, sem.at[1])]
-    for i in range(8):
-        rows = pl.ds(i * 16, 16)
-        copies.append(pltpu.make_async_copy(y_in.at[rows], y_out.at[rows], sem.at[2 + i]))
-    for c in copies:
-        c.start()
-    for c in copies:
-        c.wait()
+def emit_kernel(y_in, logp_in, lse_in, y_out, logp_out, lse_out):
+    y_out[...] = y_in[...]
+    logp_out[...] = logp_in[...]
+    lse_out[...] = lse_in[...]
 
 
 def local_step(tok_hidden, seq_lens, k_cache, v_cache, next_tok, g_attn, w_q, b_q, w_k, b_k, w_v, b_v, w_o, g_mlp, w_gate, w_up, w_down, g_final, w_head):
@@ -548,9 +546,8 @@
     y_out, logp, lse = pl.pallas_call(
         emit_kernel,
         out_shape=(jax.ShapeDtypeStruct((ROWS, WIDTH), BF16), vec, vec),
-        in_specs=[hb] * 3,
-        out_specs=(hb, hb, hb),
-        scratch_shapes=[dma((10,))],
+        in_specs=[vm] * 3,
+        out_specs=(vm, vm, vm),
         name="emit",
     )(y_out, logp, lse)
     shape = (ROWS, SLOTS, 1, HEAD)

time: 114 us -> 96.7 us (0.85)
  Pallas kernels: 113 us -> 95.9 us
    pallas_call x1, Pallas kernels: 17.1 us -> 1.88 us  [local_step(): pl.pallas_call(emit_kernel, out_shape=(jax.ShapeDtypeStruct((ROWS, WIDTH)...]
    pallas_call x1, Pallas kernels: 71.9 us -> 69.8 us  [local_step(): pl.pallas_call(kernel, out_shape=(jax.ShapeDtypeStruct((ROWS, WIDTH), BF1...]
where the time goes in v5:
time: 96.7 us; the launch traced here: 96.6 us
  Pallas kernels  95.9 us (99%)
    pallas_call x1, Pallas kernels, local_step(): pl.pallas_call(kernel, out_shape=(jax.ShapeDtypeStruct((ROWS, WIDTH), BF1...  69.8 us
    pallas_call x1, Pallas kernels, local_step(): pl.pallas_call(attn_kernel, out_shape=(jax.ShapeDtypeStruct((NCH, ROWS, C...  24.3 us

profile of v5, /device:TPU:0, one launch (start us, length us, event | category | flops | bytes accessed | tf_op | source)
XLA Modules:
  0.0 96.6 jit_solution(11983323998290165042)
XLA Ops:
  0.6 24.3 %attention.1 = (bf16[8,128,256]{2,1,0:T(8,128)(2,1)}, bf16[128,512,128]{2,1,0:T(8,128)(2,1)}, bf16[128,512,128]{2,1,0:T(8,128)(2,1)}) custom-call(s32[128]{0:T(128)} %lens_ref.1, s32[1,128]{1,0:T(1,128)} %bitcast.18, f32[1,128]{1,0:T(1,128)} %constant.2.clone.freq_hbm, bf16[128,2048]{1,0:T(8,128)(2,1)} %refs_1_.1, bf16[2048]{0:T(1024)(128)(2,1)} %g_hbm.1, ...), custom_call_target="tpu_custom_call" | custom-call | tf_op jit(solution)/shard_map/attention/pallas_call | solution.py:500
  24.9 69.8 %tail.1 = (bf16[128,2048]{1,0:T(8,128)(2,1)}, f32[1,128]{1,0:T(1,128)}, f32[1,128]{1,0:T(1,128)}) custom-call(bf16[8,128,256]{2,1,0:T(8,128)(2,1)} %get-tuple-element.14.refs_0_, bf16[128,2048]{1,0:T(8,128)(2,1)} %refs_1_.1, bf16[2048]{0:T(1024)(128)(2,1)} %refs_2_.1, bf16[2048]{0:T(1024)(128)(2,1)} %refs_3_.1, s32[1,128]{1,0:T(1,128)} %bitcast.19, ...), custom_call_target="tpu_custom_call" | custom-call | tf_op jit(solution)/shard_map/tail/pallas_call | solution.py:529
  94.7 1.9 %emit.1 = (bf16[128,2048]{1,0:T(8,128)(2,1)}, f32[1,128]{1,0:T(1,128)}, f32[1,128]{1,0:T(1,128)}) custom-call(bf16[128,2048]{1,0:T(8,128)(2,1)} %get-tuple-element.15.y_in, f32[1,128]{1,0:T(1,128)} %get-tuple-element.16.logp_in, f32[1,128]{1,0:T(1,128)} %get-tuple-element.17.lse_in), custom_call_target="tpu_custom_call" | custom-call | tf_op jit(solution)/shard_map/emit/pallas_call | solution.py:546

commit v6 on v5

--- a/solution.py
+++ b/solution.py
@@ -22,8 +22,8 @@
 NCH = 8
 HALF = 4
 BLOCK = 256
-SUM1 = ((0, 2), (2, 2))
-SUM2 = ((0, 2), (2, 1), (3, 1))
+SUM1 = ((0, 1), (1, 1), (2, 1), (3, 1))
+SUM2 = ((0, 1), (1, 1), (2, 1), (3, 1))
 TILE = 768
 RING = 18
 STEP = 4
@@ -57,9 +57,9 @@
             rows = pl.ds(g * GROUP + i * part, part)
             pltpu.make_async_copy(hbm.at[rows], buf.at[rows], sem.at[g]).start()
 
-    start_in(0, k_hbm, kbuf, ksem)
     for c in small:
         c.wait()
+    start_in(0, k_hbm, kbuf, ksem)
     start_in(0, v_hbm, vbuf, vsem)
     len_rows = jnp.broadcast_to(lenv_ref[...].astype(F32), (ROWS, ROWS)).T
     angles = len_rows * freq_ref[...]
@@ -124,8 +124,7 @@
 
         @pl.when(g + 1 == groups)
         def _():
-            for i in range(groups - 1):
-                start_out(i)
+            start_out(groups - 2)
             pltpu.make_async_copy(kbuf.at[rows], ko_hbm.at[rows], kosem.at[g]).start()
 
         for h in range(4):
@@ -159,6 +158,11 @@
         def _():
             start_in(g + 2, k_hbm, kbuf, ksem)
 
+        @pl.when(g + 2 == groups)
+        def _():
+            for i in range(groups - 2):
+                start_out(i)
+
         put(v_s, vbuf)
 
         @pl.when(g + 1 == groups)
@@ -196,7 +200,7 @@
 def tail_kernel(ff, vocab_loc,
                 part_hbm, x_hbm, gm_hbm, gf_hbm, tok_hbm, wg_hbm, wu_hbm, wd_hbm, wh_hbm,
                 y_ref, logp_ref, lse_ref,
-                part_ref, x_ref, gm_ref, gf_ref, tok_ref, wbuf, r1, s1, r2, a_s, m_s, hid, p2, r1b, s2, r2b, y_s, f_s, tok2, st_s, st_r,
+                part_ref, x_ref, gm_ref, gf_ref, tok_ref, wbuf, r1, s1, r2, a_s, m_s, hid, p2, r1b, s2, r2b, y_s, f_s, tok2, st_s, st_r, late0, late1,
                 wsem, s_d1, r_d1, s_x1, r_x1, s_a, r_a, s_d2, r_d2, s_x2, r_x2,
                 s_y, r_y, s_o, r_o, s_f, r_f, s_t, r_t, s_st, r_st, insem, ysem):
     dp = lax.axis_index('dp')
@@ -300,7 +304,7 @@
     issue(2)
     for i, (first, n) in enumerate(SUM1):
         x1[i].wait_recv()
-        issue(3)
+        issue(1 if i % 2 else 2)
         for j in range(first, first + n):
             total = s1[j].astype(F32) + r2[j].astype(F32)
             a_s[mine + j] = (x_ref[:, cols_of(mine + j)].astype(F32) + total).astype(BF16)
@@ -322,15 +326,15 @@
         cols = slice(c * CHUNK, (c + 1) * CHUNK)
         m_s[:, cols] = (a_s[c].astype(F32) * inv * gm[:, cols]).astype(BF16)
 
+    for i in range(2 * n_mlp):
+        mlp_copy(i).wait()
     for i, (r, n) in enumerate(mlp_tiles):
-        mlp_copy(2 * i).wait()
-        mlp_copy(2 * i + 1).wait()
         gslot, uslot = (2 * i) % RING, (2 * i + 1) % RING
         pad = -(-n // BLOCK) * BLOCK
         for b in range(0, pad, BLOCK):
-            gate = dot_t(m_s[...], wbuf[gslot, b:b + BLOCK, :])
-            up = dot_t(m_s[...], wbuf[uslot, b:b + BLOCK, :])
-            hid[:, r + b:r + b + BLOCK] = (gate * jax.nn.sigmoid(gate) * up).astype(BF16)
+            gate = dot_t(wbuf[gslot, b:b + BLOCK, :], m_s[...])
+            up = dot_t(wbuf[uslot, b:b + BLOCK, :], m_s[...])
+            hid[:, r + b:r + b + BLOCK] = (gate * jax.nn.sigmoid(gate) * up).T.astype(BF16)
             issue(1, 2 * i)
 
     for i in range(n_mlp):
@@ -375,9 +379,8 @@
             y_s[0, mine + j] = (a_s[mine + j].astype(F32) + total).astype(BF16)
         yy[i].start()
         yo[i].start()
-        if i:
-            forward(i - 1)
-    forward(len(SUM2) - 1)
+    for i in range(len(SUM2)):
+        forward(i)
     for c in yo:
         c.wait_recv()
     issue(RING, 3 * n_mlp)
@@ -402,10 +405,9 @@
     tok = jnp.concatenate([tok_ref[...], tok2[...]], axis=1) - (tp * vocab_loc + vbase)
     row_id = lax.broadcasted_iota(jnp.int32, (8, 2 * ROWS), 0)
 
-    def score(slot, at, size, first, state):
+    def tally(logits, first, state):
         top, tot, tgt = state
-        logits = dot_t(wbuf[slot, pl.ds(at, size), :], f_s[...])
-        blocks = [logits[8 * i:8 * i + 8] for i in range(size // 8)]
+        blocks = [logits[8 * i:8 * i + 8] for i in range(logits.shape[0] // 8)]
         peak = blocks[0]
         for v in blocks[1:]:
             peak = jnp.maximum(peak, v)
@@ -418,31 +420,48 @@
         tot = tot * jnp.exp(top - new) + part_sum
         return new, tot, tgt
 
+    def late(k, state):
+        end = (k + 1) * STEP * TILE
+        for i, ref in enumerate((late0, late1)):
+            state = tally(ref[...], jnp.where(k < 0, -(2 ** 30), end - (2 - i) * BLOCK), state)
+        return state
+
     def some_tiles(k, state):
         for t in range(STEP):
             head_copy(k * STEP + t).wait()
-        for t in range(STEP):
+        state = late(k - 1, state)
+        todo = [(t, b) for t in range(STEP) for b in range(0, TILE, BLOCK)]
+        for n, (t, b) in enumerate(todo):
             i = k * STEP + t
-            for b in range(0, TILE, BLOCK):
-                state = score(lax.rem(head0 + i, RING), b, BLOCK, i * TILE + b, state)
+            logits = dot_t(wbuf[lax.rem(head0 + i, RING), pl.ds(b, BLOCK), :], f_s[...])
+            if n < len(todo) - 2:
+                state = tally(logits, i * TILE + b, state)
+            elif n == len(todo) - 2:
+                late0[...] = logits
+            else:
+                late1[...] = logits
         for t in range(STEP):
             i = k * STEP + t
 
             @pl.when(i + RING < n_full)
             def _():
                 head_copy(i + RING).start()
-            if n_tail:
-                @pl.when(i + RING == n_full)
-                def _():
-                    head_copy(n_full, n_tail).start()
+
+            @pl.when(i + RING == n_full)
+            def _():
+                head_copy(n_full, n_tail).start()
         return state
 
+    late0[...] = jnp.full(late0.shape, -1e30, F32)
+    late1[...] = jnp.full(late1.shape, -1e30, F32)
     state = (jnp.full((8, 2 * ROWS), -1e30, F32), jnp.zeros((8, 2 * ROWS), F32), jnp.zeros((8, 2 * ROWS), F32))
     state = lax.fori_loop(0, n_full // STEP, some_tiles, state)
     head_copy(n_full, n_tail).wait()
     cut = -(-n_tail // 32) * 16
+    state = late(n_full // STEP - 1, state)
     for b, size in ((0, cut), (cut, n_tail - cut)):
-        state = score((head0 + n_full) % RING, b, size, n_full * TILE + b, state)
+        logits = dot_t(wbuf[(head0 + n_full) % RING, pl.ds(b, size), :], f_s[...])
+        state = tally(logits, n_full * TILE + b, state)
     top, tot, tgt = state
     peak = jnp.max(top, axis=0, keepdims=True)
     tot = jnp.sum(tot * jnp.exp(top - peak), axis=0, keepdims=True)
@@ -537,6 +556,7 @@
             chunk4, chunk4, chunk4, chunk8, pltpu.VMEM((ROWS, WIDTH), BF16), pltpu.VMEM((ROWS, ff_pad), BF16),
             chunk8, chunk4, chunk4, chunk4, pltpu.VMEM((2, NCH, ROWS, CHUNK), BF16), pltpu.VMEM((2 * ROWS, WIDTH), BF16),
             pltpu.VMEM((1, ROWS), jnp.int32), pltpu.VMEM((2, 8, ROWS), F32), pltpu.VMEM((8, 8, ROWS), F32),
+            pltpu.VMEM((BLOCK, 2 * ROWS), F32), pltpu.VMEM((BLOCK, 2 * ROWS), F32),
             dma((RING,)),
         ] + [dma((HALF,))] * 16 + [dma, dma, dma((7,)), dma((7,)), dma((5,)), dma((NCH,))],
         compiler_params=pltpu.CompilerParams(vmem_limit_bytes=VMEM_BYTES, collective_id=0, has_side_effects=True),

time: 96.7 us -> 90.7 us (0.938)
  Pallas kernels: 95.9 us -> 89.8 us
    pallas_call x1, Pallas kernels: 69.8 us -> 63.7 us  [local_step(): pl.pallas_call(kernel, out_shape=(jax.ShapeDtypeStruct((ROWS, WIDTH), BF1...]
where the time goes in v6:
time: 90.7 us; the launch traced here: 90.5 us
  Pallas kernels  89.8 us (99%)
    pallas_call x1, Pallas kernels, local_step(): pl.pallas_call(kernel, out_shape=(jax.ShapeDtypeStruct((ROWS, WIDTH), BF1...  63.7 us
    pallas_call x1, Pallas kernels, local_step(): pl.pallas_call(attn_kernel, out_shape=(jax.ShapeDtypeStruct((NCH, ROWS, C...  24.2 us
    pallas_call x1, Pallas kernels, local_step(): pl.pallas_call(emit_kernel, out_shape=(jax.ShapeDtypeStruct((ROWS, WIDTH)...  1.88 us

profile of v6, /device:TPU:0, one launch (start us, length us, event | category | flops | bytes accessed | tf_op | source)
XLA Modules:
  0.0 90.5 jit_solution(14125503644826371173)
XLA Ops:
  0.6 24.2 %attention.1 = (bf16[8,128,256]{2,1,0:T(8,128)(2,1)}, bf16[128,512,128]{2,1,0:T(8,128)(2,1)}, bf16[128,512,128]{2,1,0:T(8,128)(2,1)}) custom-call(s32[128]{0:T(128)} %lens_ref.1, s32[1,128]{1,0:T(1,128)} %bitcast.18, f32[1,128]{1,0:T(1,128)} %constant.2.clone.freq_hbm, bf16[128,2048]{1,0:T(8,128)(2,1)} %refs_1_.1, bf16[2048]{0:T(1024)(128)(2,1)} %g_hbm.1, ...), custom_call_target="tpu_custom_call" | custom-call | tf_op jit(solution)/shard_map/attention/pallas_call | solution.py:519
  24.9 63.7 %tail.1 = (bf16[128,2048]{1,0:T(8,128)(2,1)}, f32[1,128]{1,0:T(1,128)}, f32[1,128]{1,0:T(1,128)}) custom-call(bf16[8,128,256]{2,1,0:T(8,128)(2,1)} %get-tuple-element.14.refs_0_, bf16[128,2048]{1,0:T(8,128)(2,1)} %refs_1_.1, bf16[2048]{0:T(1024)(128)(2,1)} %refs_2_.1, bf16[2048]{0:T(1024)(128)(2,1)} %refs_3_.1, s32[1,128]{1,0:T(1,128)} %bitcast.19, ...), custom_call_target="tpu_custom_call" | custom-call | tf_op jit(solution)/shard_map/tail/pallas_call | solution.py:548
  88.6 1.9 %emit.1 = (bf16[128,2048]{1,0:T(8,128)(2,1)}, f32[1,128]{1,0:T(1,128)}, f32[1,128]{1,0:T(1,128)}) custom-call(bf16[128,2048]{1,0:T(8,128)(2,1)} %get-tuple-element.15.y_in, f32[1,128]{1,0:T(1,128)} %get-tuple-element.16.logp_in, f32[1,128]{1,0:T(1,128)} %get-tuple-element.17.lse_in), custom_call_target="tpu_custom_call" | custom-call | tf_op jit(solution)/shard_map/emit/pallas_call | solution.py:566

commit v7 on v6

--- a/solution.py
+++ b/solution.py
@@ -11,7 +11,8 @@
 MESH = pl.DeviceIdType.MESH
 F32 = jnp.float32
 BF16 = jnp.bfloat16
-VMEM_BYTES = 67043328
+ATTN_BYTES = 62 * 2 ** 20
+TAIL_BYTES = 65500000
 
 ROWS = 128
 WIDTH = 2048
@@ -39,8 +40,8 @@
 
 def attn_kernel(lens_ref, lenv_hbm, freq_hbm, x_hbm, g_hbm, bq_hbm, bk_hbm, bv_hbm,
                 wq_hbm, wk_hbm, wv_hbm, wo_hbm, k_hbm, v_hbm,
-                part_hbm, ko_hbm, vo_hbm,
-                part_ref, lenv_ref, freq_ref, x_ref, g_ref, bq_ref, bk_ref, bv_ref,
+                part_ref, ko_hbm, vo_hbm,
+                lenv_ref, freq_ref, x_ref, g_ref, bq_ref, bk_ref, bv_ref,
                 kbuf, vbuf, wq, wk, wv, wo, q_s, k_s, v_s, qg_s, qt_s, sc_s, pt_s, o_s, at_s, ll_s,
                 wsem, ksem, vsem, kosem, vosem, insem):
     groups = ROWS // GROUP
@@ -93,9 +94,13 @@
     row_seq = lax.broadcasted_iota(jnp.int32, (16, HEAD), 0) // 4
 
     def start_out(g):
-        rows = pl.ds(g * GROUP, GROUP)
-        pltpu.make_async_copy(kbuf.at[rows], ko_hbm.at[rows], kosem.at[g]).start()
-        pltpu.make_async_copy(vbuf.at[rows], vo_hbm.at[rows], vosem.at[g]).start()
+        write(g, kbuf, ko_hbm, kosem)
+        write(g, vbuf, vo_hbm, vosem)
+
+    def write(g, buf, hbm, sem):
+        for i in range(4):
+            rows = pl.ds(g * GROUP + i * part, part)
+            pltpu.make_async_copy(buf.at[rows], hbm.at[rows], sem.at[g]).start()
 
     def one_group(g, _):
         rows = pl.ds(pl.multiple_of(g * GROUP, GROUP), GROUP)
@@ -125,7 +130,7 @@
         @pl.when(g + 1 == groups)
         def _():
             start_out(groups - 2)
-            pltpu.make_async_copy(kbuf.at[rows], ko_hbm.at[rows], kosem.at[g]).start()
+            write(g, kbuf, ko_hbm, kosem)
 
         for h in range(4):
             qg_s[pl.ds(h, GROUP, stride=4), :] = q_s[h, rows, :]
@@ -167,7 +172,7 @@
 
         @pl.when(g + 1 == groups)
         def _():
-            pltpu.make_async_copy(vbuf.at[rows], vo_hbm.at[rows], vosem.at[g]).start()
+            write(g, vbuf, vo_hbm, vosem)
 
         for j in range(GROUP // 4):
             b = g * GROUP + 4 * j
@@ -188,9 +193,6 @@
     attn = at_s[...]
     for c in range(WIDTH // BLOCK):
         part_ref[c] = dot(attn, wo[:, c * BLOCK:(c + 1) * BLOCK]).astype(BF16)
-    part_copy = pltpu.make_async_copy(part_ref, part_hbm, insem.at[7])
-    part_copy.start()
-    part_copy.wait()
     for g in range(groups):
         rows = pl.ds(g * GROUP, GROUP)
         pltpu.make_async_copy(kbuf.at[rows], ko_hbm.at[rows], kosem.at[g]).wait()
@@ -198,11 +200,11 @@
 
 
 def tail_kernel(ff, vocab_loc,
-                part_hbm, x_hbm, gm_hbm, gf_hbm, tok_hbm, wg_hbm, wu_hbm, wd_hbm, wh_hbm,
+                part_ref, x_hbm, gm_hbm, gf_hbm, tok_hbm, wg_hbm, wu_hbm, wd_hbm, wh_hbm,
                 y_ref, logp_ref, lse_ref,
-                part_ref, x_ref, gm_ref, gf_ref, tok_ref, wbuf, r1, s1, r2, a_s, m_s, hid, p2, r1b, s2, r2b, y_s, f_s, tok2, st_s, st_r, late0, late1,
+                x_ref, gm_ref, gf_ref, tok_ref, wbuf, r1, s1, r2, a_s, m_s, hid, p2, r1b, s2, r2b, y_s, f_s, tok2, st_s, st_r, late0, late1,
                 wsem, s_d1, r_d1, s_x1, r_x1, s_a, r_a, s_d2, r_d2, s_x2, r_x2,
-                s_y, r_y, s_o, r_o, s_f, r_f, s_t, r_t, s_st, r_st, insem, ysem):
+                s_y, r_y, s_o, r_o, s_f, r_f, s_t, r_t, s_st, r_st, insem):
     dp = lax.axis_index('dp')
     tp = lax.axis_index('tp')
     core = lax.rem(tp, 2)
@@ -246,7 +248,7 @@
             head_copy(i - head0, n_tail).start()
 
     small = [pltpu.make_async_copy(src, dst, insem.at[i]) for i, (src, dst) in enumerate((
-        (part_hbm, part_ref), (x_hbm, x_ref), (gm_hbm, gm_ref), (gf_hbm, gf_ref), (tok_hbm, tok_ref)))]
+        (x_hbm, x_ref), (gm_hbm, gm_ref), (gf_hbm, gf_ref), (tok_hbm, tok_ref)))]
     for c in small:
         c.start()
     issued = [0]
@@ -269,8 +271,6 @@
     if tail_pad > last_n:
         for i in (2 * n_mlp - 2, 2 * n_mlp - 1, 3 * n_mlp - 1):
             wbuf[i % RING, last_n:tail_pad, :] = jnp.zeros((tail_pad - last_n, WIDTH), BF16)
-    for c in small:
-        c.wait()
     pl.semaphore_wait(barrier, 7)
     issue(2)
 
@@ -295,6 +295,8 @@
 
     for c in d1:
         c.start()
+    for c in small:
+        c.wait()
     tok_copy.start()
     for i, (first, n) in enumerate(SUM1):
         d1[i].wait_recv()
@@ -384,9 +386,8 @@
     for c in yo:
         c.wait_recv()
     issue(RING, 3 * n_mlp)
-    y_out = [pltpu.make_async_copy(y_s.at[0, c], y_ref.at[:, pl.ds(c * CHUNK, CHUNK)], ysem.at[c]) for c in range(NCH)]
-    for c in y_out:
-        c.start()
+    for c in range(NCH):
+        y_ref[:, c * CHUNK:(c + 1) * CHUNK] = y_s[0, c]
 
     gf = gf_ref[...].astype(F32).reshape(1, WIDTH)
 
@@ -498,14 +499,14 @@
     for group in (d1, x1, ac, d2, x2, yo, yy, yf):
         for c in group:
             c.wait_send()
-    for c in y_out:
+
+
+def emit_kernel(y_in, logp_in, lse_in, y_out, logp_out, lse_out, sem):
+    copies = [pltpu.make_async_copy(src, dst, sem.at[i]) for i, (src, dst) in enumerate(((y_in, y_out), (logp_in, logp_out), (lse_in, lse_out)))]
+    for c in copies:
+        c.start()
+    for c in copies:
         c.wait()
-
-
-def emit_kernel(y_in, logp_in, lse_in, y_out, logp_out, lse_out):
-    y_out[...] = y_in[...]
-    logp_out[...] = logp_in[...]
-    lse_out[...] = lse_in[...]
 
 
 def local_step(tok_hidden, seq_lens, k_cache, v_cache, next_tok, g_attn, w_q, b_q, w_k, b_k, w_v, b_v, w_o, g_mlp, w_gate, w_up, w_down, g_final, w_head):
@@ -518,20 +519,20 @@
     cache = jax.ShapeDtypeStruct((ROWS, SLOTS, HEAD), BF16)
     part, k_all, v_all = pl.pallas_call(
         attn_kernel,
-        out_shape=(jax.ShapeDtypeStruct((NCH, ROWS, CHUNK), BF16), cache, cache),
+        out_shape=(pltpu.VMEM((NCH, ROWS, CHUNK), BF16), cache, cache),
         in_specs=[sm] + [hb] * 13,
-        out_specs=(hb, hb, hb),
+        out_specs=(vm, hb, hb),
         scratch_shapes=[
-            pltpu.VMEM((NCH, ROWS, CHUNK), BF16), pltpu.VMEM((1, ROWS), jnp.int32), pltpu.VMEM((1, HEAD), F32), pltpu.VMEM((ROWS, WIDTH), BF16), pltpu.VMEM((WIDTH,), BF16),
+            pltpu.VMEM((1, ROWS), jnp.int32), pltpu.VMEM((1, HEAD), F32), pltpu.VMEM((ROWS, WIDTH), BF16), pltpu.VMEM((WIDTH,), BF16),
             pltpu.VMEM((4 * HEAD,), BF16), pltpu.VMEM((HEAD,), BF16), pltpu.VMEM((HEAD,), BF16),
             pltpu.VMEM((ROWS, SLOTS, HEAD), BF16), pltpu.VMEM((ROWS, SLOTS, HEAD), BF16),
             pltpu.VMEM((WIDTH, 512), BF16), pltpu.VMEM((WIDTH, HEAD), BF16), pltpu.VMEM((WIDTH, HEAD), BF16), pltpu.VMEM((512, WIDTH), BF16),
             pltpu.VMEM((4, ROWS, HEAD), F32), pltpu.VMEM((ROWS, HEAD), F32), pltpu.VMEM((ROWS, HEAD), F32),
             pltpu.VMEM((128, HEAD), F32), pltpu.VMEM((HEAD, 128), BF16), pltpu.VMEM((SLOTS, 128), F32), pltpu.VMEM((128, SLOTS), BF16),
             pltpu.VMEM((128, HEAD), F32), pltpu.VMEM((ROWS, 512), BF16), pltpu.VMEM((8, 128), jnp.int32),
-            dma((4,)), dma((4,)), dma((4,)), dma((4,)), dma((4,)), dma((8,)),
+            dma((4,)), dma((4,)), dma((4,)), dma((4,)), dma((4,)), dma((7,)),
         ],
-        compiler_params=pltpu.CompilerParams(vmem_limit_bytes=VMEM_BYTES),
+        compiler_params=pltpu.CompilerParams(vmem_limit_bytes=ATTN_BYTES),
         name="attention",
     )(seq_lens, seq_lens.reshape(1, ROWS), freq, tok_hidden, g_attn, b_q, b_k, b_v,
       w_q, w_k, w_v, w_o, k_cache.reshape(ROWS, SLOTS, HEAD), v_cache.reshape(ROWS, SLOTS, HEAD))
@@ -547,29 +548,30 @@
 
     y_out, logp, lse = pl.pallas_call(
         kernel,
-        out_shape=(jax.ShapeDtypeStruct((ROWS, WIDTH), BF16), jax.ShapeDtypeStruct((1, ROWS), F32), jax.ShapeDtypeStruct((1, ROWS), F32)),
-        in_specs=[hb] * 9,
-        out_specs=(hb, vm, vm),
+        out_shape=(pltpu.VMEM((ROWS, WIDTH), BF16), pltpu.VMEM((1, ROWS), F32), pltpu.VMEM((1, ROWS), F32)),
+        in_specs=[vm] + [hb] * 8,
+        out_specs=(vm, vm, vm),
         scratch_shapes=[
-            chunk8, pltpu.VMEM((ROWS, WIDTH), BF16), pltpu.VMEM((WIDTH,), BF16), pltpu.VMEM((WIDTH,), BF16), pltpu.VMEM((1, ROWS), jnp.int32),
+            pltpu.VMEM((ROWS, WIDTH), BF16), pltpu.VMEM((WIDTH,), BF16), pltpu.VMEM((WIDTH,), BF16), pltpu.VMEM((1, ROWS), jnp.int32),
             pltpu.VMEM((RING, TILE, WIDTH), BF16),
             chunk4, chunk4, chunk4, chunk8, pltpu.VMEM((ROWS, WIDTH), BF16), pltpu.VMEM((ROWS, ff_pad), BF16),
             chunk8, chunk4, chunk4, chunk4, pltpu.VMEM((2, NCH, ROWS, CHUNK), BF16), pltpu.VMEM((2 * ROWS, WIDTH), BF16),
             pltpu.VMEM((1, ROWS), jnp.int32), pltpu.VMEM((2, 8, ROWS), F32), pltpu.VMEM((8, 8, ROWS), F32),
             pltpu.VMEM((BLOCK, 2 * ROWS), F32), pltpu.VMEM((BLOCK, 2 * ROWS), F32),
             dma((RING,)),
-        ] + [dma((HALF,))] * 16 + [dma, dma, dma((7,)), dma((7,)), dma((5,)), dma((NCH,))],
-        compiler_params=pltpu.CompilerParams(vmem_limit_bytes=VMEM_BYTES, collective_id=0, has_side_effects=True),
+        ] + [dma((HALF,))] * 16 + [dma, dma, dma((7,)), dma((7,)), dma((4,))],
+        compiler_params=pltpu.CompilerParams(vmem_limit_bytes=TAIL_BYTES, collective_id=0, has_side_effects=True),
         name="tail",
-    )(part, tok_hidden, g_mlp, g_final, next_tok.reshape(1, ROWS), w_gate.T, w_up.T, w_down, w_head)
+    )(pltpu.with_memory_space_constraint(part, pltpu.VMEM), tok_hidden, g_mlp, g_final, next_tok.reshape(1, ROWS), w_gate.T, w_up.T, w_down, w_head)
     vec = jax.ShapeDtypeStruct((1, ROWS), F32)
     y_out, logp, lse = pl.pallas_call(
         emit_kernel,
         out_shape=(jax.ShapeDtypeStruct((ROWS, WIDTH), BF16), vec, vec),
         in_specs=[vm] * 3,
-        out_specs=(vm, vm, vm),
+        out_specs=(hb, hb, hb),
+        scratch_shapes=[dma((3,))],
         name="emit",
-    )(y_out, logp, lse)
+    )(*(pltpu.with_memory_space_constraint(v, pltpu.VMEM) for v in (y_out, logp, lse)))
     shape = (ROWS, SLOTS, 1, HEAD)
     return y_out, k_all.reshape(shape), v_all.reshape(shape), logp.reshape(ROWS), lse.reshape(ROWS)
 

time: 90.7 us -> 88.1 us (0.971)
  Pallas kernels: 89.8 us -> 87.1 us
    pallas_call x2, Pallas kernels: 87.9 us -> 86.3 us  [the longest x1 62.2 us: local_step(): pl.pallas_call(kernel, out_shape=(pltpu.VMEM((ROWS, WIDTH), BF16), pltpu....]
    pallas_call x1, Pallas kernels: 1.88 us -> 0.83 us  [local_step(): pl.pallas_call(emit_kernel, out_shape=(jax.ShapeDtypeStruct((ROWS, WIDTH)...]
where the time goes in v7:
time: 88.1 us; the launch traced here: 87.9 us
  Pallas kernels  87.1 us (99%)
    pallas_call x1, Pallas kernels, local_step(): pl.pallas_call(kernel, out_shape=(pltpu.VMEM((ROWS, WIDTH), BF16), pltpu....  62.2 us
    pallas_call x1, Pallas kernels, local_step(): pl.pallas_call(attn_kernel, out_shape=(pltpu.VMEM((NCH, ROWS, CHUNK), BF1...  24.1 us

profile of v7, /device:TPU:0, one launch (start us, length us, event | category | flops | bytes accessed | tf_op | source)
XLA Modules:
  0.0 87.9 jit_solution(18413514064360349250)
XLA Ops:
  0.6 24.1 %attention.1 = (bf16[8,128,256]{2,1,0:T(8,128)(2,1)S(1)}, bf16[128,512,128]{2,1,0:T(8,128)(2,1)}, bf16[128,512,128]{2,1,0:T(8,128)(2,1)}) custom-call(s32[128]{0:T(128)} %lens_ref.1, s32[1,128]{1,0:T(1,128)} %bitcast.18, f32[1,128]{1,0:T(1,128)} %constant.2.clone.freq_hbm, bf16[128,2048]{1,0:T(8,128)(2,1)} %refs_1_.1, bf16[2048]{0:T(1024)(128)(2,1)} %g_hbm.1, ...), custom_call_target="tpu_custom_call" | custom-call | tf_op jit(solution)/shard_map/attention/pallas_call | solution.py:520
  24.7 62.2 %tail.1 = (bf16[128,2048]{1,0:T(8,128)(2,1)S(1)}, f32[1,128]{1,0:T(1,128)S(1)}, f32[1,128]{1,0:T(1,128)S(1)}) custom-call(bf16[8,128,256]{2,1,0:T(8,128)(2,1)S(1)} %get-tuple-element.14.refs_0_, bf16[128,2048]{1,0:T(8,128)(2,1)} %refs_1_.1, bf16[2048]{0:T(1024)(128)(2,1)} %refs_2_.1, bf16[2048]{0:T(1024)(128)(2,1)} %refs_3_.1, s32[1,128]{1,0:T(1,128)} %bitcast.19, ...), custom_call_target="tpu_custom_call" | custom-call | tf_op jit(solution)/shard_map/tail/pallas_call | solution.py:549
  86.9 0.8 emit.1

commit v8 on v7

--- a/solution.py
+++ b/solution.py
@@ -23,11 +23,12 @@
 NCH = 8
 HALF = 4
 BLOCK = 256
+HBLK = 192
 SUM1 = ((0, 1), (1, 1), (2, 1), (3, 1))
 SUM2 = ((0, 1), (1, 1), (2, 1), (3, 1))
 TILE = 768
 RING = 18
-STEP = 4
+STEP = 8
 
 
 def dot(a, b):
@@ -395,7 +396,7 @@
         inv = inv_rms(y_s.at[grp])
         for c in range(NCH):
             cols = slice(c * CHUNK, (c + 1) * CHUNK)
-            f_s[grp * ROWS:(grp + 1) * ROWS, cols] = (y_s[grp, c].astype(F32) * inv * gf[:, cols]).astype(BF16)
+            f_s[cols, grp * ROWS:(grp + 1) * ROWS] = (y_s[grp, c].astype(F32) * inv * gf[:, cols]).T.astype(BF16)
 
     final_norm(0)
     for c in yf:
@@ -424,17 +425,17 @@
     def late(k, state):
         end = (k + 1) * STEP * TILE
         for i, ref in enumerate((late0, late1)):
-            state = tally(ref[...], jnp.where(k < 0, -(2 ** 30), end - (2 - i) * BLOCK), state)
+            state = tally(ref[...], jnp.where(k < 0, -(2 ** 30), end - (2 - i) * HBLK), state)
         return state
 
     def some_tiles(k, state):
         for t in range(STEP):
             head_copy(k * STEP + t).wait()
         state = late(k - 1, state)
-        todo = [(t, b) for t in range(STEP) for b in range(0, TILE, BLOCK)]
+        todo = [(t, b) for t in range(STEP) for b in range(0, TILE, HBLK)]
         for n, (t, b) in enumerate(todo):
             i = k * STEP + t
-            logits = dot_t(wbuf[lax.rem(head0 + i, RING), pl.ds(b, BLOCK), :], f_s[...])
+            logits = dot(wbuf[lax.rem(head0 + i, RING), pl.ds(b, HBLK), :], f_s[...])
             if n < len(todo) - 2:
                 state = tally(logits, i * TILE + b, state)
             elif n == len(todo) - 2:
@@ -458,10 +459,10 @@
     state = (jnp.full((8, 2 * ROWS), -1e30, F32), jnp.zeros((8, 2 * ROWS), F32), jnp.zeros((8, 2 * ROWS), F32))
     state = lax.fori_loop(0, n_full // STEP, some_tiles, state)
     head_copy(n_full, n_tail).wait()
-    cut = -(-n_tail // 32) * 16
     state = late(n_full // STEP - 1, state)
-    for b, size in ((0, cut), (cut, n_tail - cut)):
-        logits = dot_t(wbuf[(head0 + n_full) % RING, pl.ds(b, size), :], f_s[...])
+    cut = -(-n_tail // 64) * 16
+    for b in range(0, n_tail, cut):
+        logits = dot(wbuf[(head0 + n_full) % RING, pl.ds(b, min(cut, n_tail - b)), :], f_s[...])
         state = tally(logits, n_full * TILE + b, state)
     top, tot, tgt = state
     peak = jnp.max(top, axis=0, keepdims=True)
@@ -555,9 +556,9 @@
             pltpu.VMEM((ROWS, WIDTH), BF16), pltpu.VMEM((WIDTH,), BF16), pltpu.VMEM((WIDTH,), BF16), pltpu.VMEM((1, ROWS), jnp.int32),
             pltpu.VMEM((RING, TILE, WIDTH), BF16),
             chunk4, chunk4, chunk4, chunk8, pltpu.VMEM((ROWS, WIDTH), BF16), pltpu.VMEM((ROWS, ff_pad), BF16),
-            chunk8, chunk4, chunk4, chunk4, pltpu.VMEM((2, NCH, ROWS, CHUNK), BF16), pltpu.VMEM((2 * ROWS, WIDTH), BF16),
+            chunk8, chunk4, chunk4, chunk4, pltpu.VMEM((2, NCH, ROWS, CHUNK), BF16), pltpu.VMEM((WIDTH, 2 * ROWS), BF16),
             pltpu.VMEM((1, ROWS), jnp.int32), pltpu.VMEM((2, 8, ROWS), F32), pltpu.VMEM((8, 8, ROWS), F32),
-            pltpu.VMEM((BLOCK, 2 * ROWS), F32), pltpu.VMEM((BLOCK, 2 * ROWS), F32),
+            pltpu.VMEM((HBLK, 2 * ROWS), F32), pltpu.VMEM((HBLK, 2 * ROWS), F32),
             dma((RING,)),
         ] + [dma((HALF,))] * 16 + [dma, dma, dma((7,)), dma((7,)), dma((4,))],
         compiler_params=pltpu.CompilerParams(vmem_limit_bytes=TAIL_BYTES, collective_id=0, has_side_effects=True),

time: 88.1 us -> 88.9 us (level)
  no operation moved by 1% of the time
where the time goes in v8:
time: 88.9 us; the launch traced here: 88.7 us
  Pallas kernels  87.9 us (99%)
    pallas_call x1, Pallas kernels, local_step(): pl.pallas_call(kernel, out_shape=(pltpu.VMEM((ROWS, WIDTH), BF16), pltpu....  63 us
    pallas_call x1, Pallas kernels, local_step(): pl.pallas_call(attn_kernel, out_shape=(pltpu.VMEM((NCH, ROWS, CHUNK), BF1...  24.1 us

profile of v8, /device:TPU:0, one launch (start us, length us, event | category | flops | bytes accessed | tf_op | source)
XLA Modules:
  0.0 88.7 jit_solution(7005241950116818924)
XLA Ops:
  0.6 24.1 %attention.1 = (bf16[8,128,256]{2,1,0:T(8,128)(2,1)S(1)}, bf16[128,512,128]{2,1,0:T(8,128)(2,1)}, bf16[128,512,128]{2,1,0:T(8,128)(2,1)}) custom-call(s32[128]{0:T(128)} %lens_ref.1, s32[1,128]{1,0:T(1,128)} %bitcast.18, f32[1,128]{1,0:T(1,128)} %constant.2.clone.freq_hbm, bf16[128,2048]{1,0:T(8,128)(2,1)} %refs_1_.1, bf16[2048]{0:T(1024)(128)(2,1)} %g_hbm.1, ...), custom_call_target="tpu_custom_call" | custom-call | tf_op jit(solution)/shard_map/attention/pallas_call | solution.py:521
  24.7 63.0 %tail.1 = (bf16[128,2048]{1,0:T(8,128)(2,1)S(1)}, f32[1,128]{1,0:T(1,128)S(1)}, f32[1,128]{1,0:T(1,128)S(1)}) custom-call(bf16[8,128,256]{2,1,0:T(8,128)(2,1)S(1)} %get-tuple-element.14.refs_0_, bf16[128,2048]{1,0:T(8,128)(2,1)} %refs_1_.1, bf16[2048]{0:T(1024)(128)(2,1)} %refs_2_.1, bf16[2048]{0:T(1024)(128)(2,1)} %refs_3_.1, s32[1,128]{1,0:T(1,128)} %bitcast.19, ...), custom_call_target="tpu_custom_call" | custom-call | tf_op jit(solution)/shard_map/tail/pallas_call | solution.py:550
  87.7 0.8 emit.1

commit v9 on v7

--- a/solution.py
+++ b/solution.py
@@ -21,12 +21,11 @@
 GROUP = 32
 CHUNK = 256
 NCH = 8
-HALF = 4
 BLOCK = 256
-SUM1 = ((0, 1), (1, 1), (2, 1), (3, 1))
-SUM2 = ((0, 1), (1, 1), (2, 1), (3, 1))
+OWN = ((0, 1, 2), (3, 4, 5, 6, 7))
+MOST = 5
 TILE = 768
-RING = 18
+RING = 17
 STEP = 4
 
 
@@ -212,8 +211,6 @@
     partner = (dp, tp + 1 - 2 * core)
     xnext = (dp, lax.rem(tp + 2, 4))
     ynext = (1 - dp, tp)
-    mine = core * HALF
-    other = (1 - core) * HALF
 
     mlp_tiles = [(i * TILE, min(TILE, ff - i * TILE)) for i in range(-(-ff // TILE))]
     n_mlp = len(mlp_tiles)
@@ -278,41 +275,56 @@
         return pltpu.make_async_remote_copy(src_ref=src, dst_ref=dst, send_sem=ssem, recv_sem=rsem, device_id=who, device_id_type=MESH)
 
     tok_copy = remote(tok_ref, tok2, s_t, r_t, ynext)
-    def part_of(ref, base, grp):
-        return ref.at[pl.ds(base + grp[0], grp[1])]
-
-    d1 = [remote(part_of(part_ref, other, p), part_of(r1, 0, p), s_d1.at[i], r_d1.at[i], partner) for i, p in enumerate(SUM1)]
-    x1 = [remote(part_of(s1, 0, p), part_of(r2, 0, p), s_x1.at[i], r_x1.at[i], xnext) for i, p in enumerate(SUM1)]
-    ac = [remote(part_of(a_s, mine, p), part_of(a_s, mine, p), s_a.at[i], r_a.at[i], partner) for i, p in enumerate(SUM1)]
-    d2 = [remote(part_of(p2, other, p), part_of(r1b, 0, p), s_d2.at[i], r_d2.at[i], partner) for i, p in enumerate(SUM2)]
-    x2 = [remote(part_of(s2, 0, p), part_of(r2b, 0, p), s_x2.at[i], r_x2.at[i], xnext) for i, p in enumerate(SUM2)]
-    yo = [remote(part_of(y_s.at[0], mine, p), part_of(y_s.at[0], mine, p), s_o.at[i], r_o.at[i], partner) for i, p in enumerate(SUM2)]
-    yy = [remote(part_of(y_s.at[0], mine, p), part_of(y_s.at[1], mine, p), s_y.at[i], r_y.at[i], ynext) for i, p in enumerate(SUM2)]
-    yf = [remote(part_of(y_s.at[1], mine, p), part_of(y_s.at[1], mine, p), s_f.at[i], r_f.at[i], partner) for i, p in enumerate(SUM2)]
-
     def cols_of(c):
-        return pl.ds(pl.multiple_of(c * CHUNK, CHUNK), CHUNK)
-
-    for c in d1:
-        c.start()
-    for c in small:
-        c.wait()
-    tok_copy.start()
-    for i, (first, n) in enumerate(SUM1):
-        d1[i].wait_recv()
-        for j in range(first, first + n):
-            s1[j] = (part_ref[mine + j].astype(F32) + r1[j].astype(F32)).astype(BF16)
-        x1[i].start()
-    issue(2)
-    for i, (first, n) in enumerate(SUM1):
-        x1[i].wait_recv()
-        issue(1 if i % 2 else 2)
-        for j in range(first, first + n):
-            total = s1[j].astype(F32) + r2[j].astype(F32)
-            a_s[mine + j] = (x_ref[:, cols_of(mine + j)].astype(F32) + total).astype(BF16)
-        ac[i].start()
-    for c in ac:
-        c.wait_recv()
+        return slice(c * CHUNK, (c + 1) * CHUNK)
+
+    def copies(o):
+        own, their = OWN[o], OWN[1 - o]
+        d1 = [remote(part_ref.at[c], r1.at[i], s_d1.at[i], r_d1.at[i], partner) for i, c in enumerate(their)]
+        x1 = [remote(s1.at[i], r2.at[i], s_x1.at[i], r_x1.at[i], xnext) for i, c in enumerate(own)]
+        ac = [remote(a_s.at[c], a_s.at[c], s_a.at[i], r_a.at[i], partner) for i, c in enumerate(own)]
+        d2 = [remote(p2.at[c], r1b.at[i], s_d2.at[i], r_d2.at[i], partner) for i, c in enumerate(their)]
+        x2 = [remote(s2.at[i], r2b.at[i], s_x2.at[i], r_x2.at[i], xnext) for i, c in enumerate(own)]
+        yo = [remote(y_s.at[0, c], y_s.at[0, c], s_o.at[i], r_o.at[i], partner) for i, c in enumerate(own)]
+        yy = [remote(y_s.at[0, c], y_s.at[1, c], s_y.at[i], r_y.at[i], ynext) for i, c in enumerate(own)]
+        yf = [remote(y_s.at[1, c], y_s.at[1, c], s_f.at[i], r_f.at[i], partner) for i, c in enumerate(own)]
+        return d1, x1, ac, d2, x2, yo, yy, yf
+
+    def per_core(run):
+        before = issued[0]
+        for o in range(2):
+            issued[0] = before
+
+            @pl.when(core == o)
+            def _():
+                run(o)
+
+    def first_sum(o):
+        own, their = OWN[o], OWN[1 - o]
+        d1, x1, ac = copies(o)[:3]
+        arrive = [c for c in copies(1 - o)[0]]
+        back = copies(1 - o)[2]
+        for c in d1:
+            c.start()
+        for i, c in enumerate(own):
+            arrive[i].wait_recv()
+            s1[i] = (part_ref[c].astype(F32) + r1[i].astype(F32)).astype(BF16)
+            x1[i].start()
+        issue(2)
+        for c in small:
+            c.wait()
+        tok_copy.start()
+        for i, c in enumerate(own):
+            x1[i].wait_recv()
+            issue(min(6 // len(own), 12 - issued[0]))
+            total = s1[i].astype(F32) + r2[i].astype(F32)
+            a_s[c] = (x_ref[:, cols_of(c)].astype(F32) + total).astype(BF16)
+            ac[i].start()
+        issue(12 - issued[0])
+        for i in range(len(their)):
+            back[i].wait_recv()
+
+    per_core(first_sum)
     issue(1)
 
     def inv_rms(src):
@@ -350,42 +362,48 @@
             acc = term if acc is None else acc + term
         return acc.astype(BF16)
 
-    def chip_sum(i):
-        d2[i].wait_recv()
-        first, n = SUM2[i]
-        for j in range(first, first + n):
-            s2[j] = (p2[mine + j].astype(F32) + r1b[j].astype(F32)).astype(BF16)
-        x2[i].start()
-
-    for i, (first, n) in enumerate(SUM2):
-        for j in range(first, first + n):
-            theirs, ours = down(other + j), down(mine + j)
-            p2[other + j] = theirs
-            p2[mine + j] = ours
+    def second_sum(o):
+        own, their = OWN[o], OWN[1 - o]
+        _, _, _, d2, x2, yo, yy, yf = copies(o)
+        arrive, back = copies(1 - o)[3], copies(1 - o)[5]
+
+        def chip_sum(i):
+            arrive[i].wait_recv()
+            s2[i] = (p2[own[i]].astype(F32) + r1b[i].astype(F32)).astype(BF16)
+            x2[i].start()
+
+        both = min(len(own), len(their))
+        rest = (own + their)[both:len(own)] if len(own) > both else their[both:]
+        steps = [(their[i], own[i]) for i in range(both)] + [tuple(rest)]
+        summed = 0
+        for n, pair in enumerate(steps):
+            for c, val in zip(pair, [down(c) for c in pair]):
+                p2[c] = val
+            for c in pair:
+                if c in their:
+                    d2[their.index(c)].start()
             issue(1, 2 * n_mlp)
-        d2[i].start()
-        if i:
-            chip_sum(i - 1)
-    chip_sum(len(SUM2) - 1)
-    issue(1, 3 * n_mlp)
-
-    def forward(i):
-        yy[i].wait_recv()
-        yf[i].start()
-
-    for i, (first, n) in enumerate(SUM2):
-        x2[i].wait_recv()
-        issue(2, 3 * n_mlp)
-        for j in range(first, first + n):
-            total = s2[j].astype(F32) + r2b[j].astype(F32)
-            y_s[0, mine + j] = (a_s[mine + j].astype(F32) + total).astype(BF16)
-        yy[i].start()
-        yo[i].start()
-    for i in range(len(SUM2)):
-        forward(i)
-    for c in yo:
-        c.wait_recv()
-    issue(RING, 3 * n_mlp)
+            if n and summed < len(own):
+                chip_sum(summed)
+                summed += 1
+        for i in range(summed, len(own)):
+            chip_sum(i)
+        issue(1, 3 * n_mlp)
+        for i, c in enumerate(own):
+            x2[i].wait_recv()
+            issue(2, 3 * n_mlp)
+            total = s2[i].astype(F32) + r2b[i].astype(F32)
+            y_s[0, c] = (a_s[c].astype(F32) + total).astype(BF16)
+            yy[i].start()
+            yo[i].start()
+        for i in range(len(own)):
+            yy[i].wait_recv()
+            yf[i].start()
+        issue(RING, 3 * n_mlp)
+        for i in range(len(their)):
+            back[i].wait_recv()
+
+    per_core(second_sum)
     for c in range(NCH):
         y_ref[:, c * CHUNK:(c + 1) * CHUNK] = y_s[0, c]
 
@@ -398,8 +416,12 @@
             f_s[grp * ROWS:(grp + 1) * ROWS, cols] = (y_s[grp, c].astype(F32) * inv * gf[:, cols]).astype(BF16)
 
     final_norm(0)
-    for c in yf:
-        c.wait_recv()
+
+    def forwarded(o):
+        for c in copies(1 - o)[7]:
+            c.wait_recv()
+
+    per_core(forwarded)
     final_norm(1)
     tok_copy.wait()
 
@@ -496,9 +518,12 @@
     lse_ref[...] = lse
     logp_ref[...] = tgt - lse
 
-    for group in (d1, x1, ac, d2, x2, yo, yy, yf):
-        for c in group:
-            c.wait_send()
+    def sent(o):
+        for group in copies(o):
+            for c in group:
+                c.wait_send()
+
+    per_core(sent)
 
 
 def emit_kernel(y_in, logp_in, lse_in, y_out, logp_out, lse_out, sem):
@@ -540,7 +565,7 @@
     ff = w_gate.shape[1]
     vocab_loc = w_head.shape[0]
     ff_pad = -(-ff // BLOCK) * BLOCK
-    chunk4 = pltpu.VMEM((HALF, ROWS, CHUNK), BF16)
+    some = pltpu.VMEM((MOST, ROWS, CHUNK), BF16)
     chunk8 = pltpu.VMEM((NCH, ROWS, CHUNK), BF16)
 
     def kernel(*refs):
@@ -554,12 +579,12 @@
         scratch_shapes=[
             pltpu.VMEM((ROWS, WIDTH), BF16), pltpu.VMEM((WIDTH,), BF16), pltpu.VMEM((WIDTH,), BF16), pltpu.VMEM((1, ROWS), jnp.int32),
             pltpu.VMEM((RING, TILE, WIDTH), BF16),
-            chunk4, chunk4, chunk4, chunk8, pltpu.VMEM((ROWS, WIDTH), BF16), pltpu.VMEM((ROWS, ff_pad), BF16),
-            chunk8, chunk4, chunk4, chunk4, pltpu.VMEM((2, NCH, ROWS, CHUNK), BF16), pltpu.VMEM((2 * ROWS, WIDTH), BF16),
+            some, some, some, chunk8, pltpu.VMEM((ROWS, WIDTH), BF16), pltpu.VMEM((ROWS, ff_pad), BF16),
+            chunk8, some, some, some, pltpu.VMEM((2, NCH, ROWS, CHUNK), BF16), pltpu.VMEM((2 * ROWS, WIDTH), BF16),
             pltpu.VMEM((1, ROWS), jnp.int32), pltpu.VMEM((2, 8, ROWS), F32), pltpu.VMEM((8, 8, ROWS), F32),
             pltpu.VMEM((BLOCK, 2 * ROWS), F32), pltpu.VMEM((BLOCK, 2 * ROWS), F32),
             dma((RING,)),
-        ] + [dma((HALF,))] * 16 + [dma, dma, dma((7,)), dma((7,)), dma((4,))],
+        ] + [dma((MOST,))] * 16 + [dma, dma, dma((7,)), dma((7,)), dma((4,))],
         compiler_params=pltpu.CompilerParams(vmem_limit_bytes=TAIL_BYTES, collective_id=0, has_side_effects=True),
         name="tail",
     )(pltpu.with_memory_space_constraint(part, pltpu.VMEM), tok_hidden, g_mlp, g_final, next_tok.reshape(1, ROWS), w_gate.T, w_up.T, w_down, w_head)

time: 88.1 us -> 88.1 us (level)
  no operation moved by 1% of the time
where the time goes in v9:
time: 88.1 us; the launch traced here: 88 us
  Pallas kernels  87.2 us (99%)
    pallas_call x1, Pallas kernels, local_step(): pl.pallas_call(kernel, out_shape=(pltpu.VMEM((ROWS, WIDTH), BF16), pltpu....  62.3 us
    pallas_call x1, Pallas kernels, local_step(): pl.pallas_call(attn_kernel, out_shape=(pltpu.VMEM((NCH, ROWS, CHUNK), BF1...  24.1 us

profile of v9, /device:TPU:0, one launch (start us, length us, event | category | flops | bytes accessed | tf_op | source)
XLA Modules:
  0.0 88.0 jit_solution(5654456256964267544)
XLA Ops:
  0.6 24.1 %attention.1 = (bf16[8,128,256]{2,1,0:T(8,128)(2,1)S(1)}, bf16[128,512,128]{2,1,0:T(8,128)(2,1)}, bf16[128,512,128]{2,1,0:T(8,128)(2,1)}) custom-call(s32[128]{0:T(128)} %lens_ref.1, s32[1,128]{1,0:T(1,128)} %bitcast.18, f32[1,128]{1,0:T(1,128)} %constant.2.clone.freq_hbm, bf16[128,2048]{1,0:T(8,128)(2,1)} %refs_1_.1, bf16[2048]{0:T(1024)(128)(2,1)} %g_hbm.1, ...), custom_call_target="tpu_custom_call" | custom-call | tf_op jit(solution)/shard_map/attention/pallas_call | solution.py:545
  24.7 62.3 %tail.1 = (bf16[128,2048]{1,0:T(8,128)(2,1)S(1)}, f32[1,128]{1,0:T(1,128)S(1)}, f32[1,128]{1,0:T(1,128)S(1)}) custom-call(bf16[8,128,256]{2,1,0:T(8,128)(2,1)S(1)} %get-tuple-element.14.refs_0_, bf16[128,2048]{1,0:T(8,128)(2,1)} %refs_1_.1, bf16[2048]{0:T(1024)(128)(2,1)} %refs_2_.1, bf16[2048]{0:T(1024)(128)(2,1)} %refs_3_.1, s32[1,128]{1,0:T(1,128)} %bitcast.19, ...), custom_call_target="tpu_custom_call" | custom-call | tf_op jit(solution)/shard_map/tail/pallas_call | solution.py:574
  87.0 0.8 emit.1

commit v10 on v7

--- a/solution.py
+++ b/solution.py
@@ -53,14 +53,15 @@
     for i, (src, dst) in enumerate(((wq_hbm, wq), (wk_hbm, wk), (wv_hbm, wv))):
         pltpu.make_async_copy(src, dst, wsem.at[i]).start()
 
-    def start_in(g, hbm, buf, sem):
-        for i in range(4):
+    def start_in(g, hbm, buf, sem, lo=0, hi=4):
+        for i in range(lo, hi):
             rows = pl.ds(g * GROUP + i * part, part)
             pltpu.make_async_copy(hbm.at[rows], buf.at[rows], sem.at[g]).start()
 
+    start_in(0, k_hbm, kbuf, ksem, 0, 2)
     for c in small:
         c.wait()
-    start_in(0, k_hbm, kbuf, ksem)
+    start_in(0, k_hbm, kbuf, ksem, 2, 4)
     start_in(0, v_hbm, vbuf, vsem)
     len_rows = jnp.broadcast_to(lenv_ref[...].astype(F32), (ROWS, ROWS)).T
     angles = len_rows * freq_ref[...]

time: 88.1 us -> 87.9 us (level)
  no operation moved by 1% of the time
where the time goes in v10:
time: 87.9 us; the launch traced here: 87.7 us
  Pallas kernels  86.9 us (99%)
    pallas_call x1, Pallas kernels, local_step(): pl.pallas_call(kernel, out_shape=(pltpu.VMEM((ROWS, WIDTH), BF16), pltpu....  62.2 us
    pallas_call x1, Pallas kernels, local_step(): pl.pallas_call(attn_kernel, out_shape=(pltpu.VMEM((NCH, ROWS, CHUNK), BF1...  23.9 us

profile of v10, /device:TPU:0, one launch (start us, length us, event | category | flops | bytes accessed | tf_op | source)
XLA Modules:
  0.0 87.7 jit_solution(10634547759271548604)
XLA Ops:
  0.6 23.9 %attention.1 = (bf16[8,128,256]{2,1,0:T(8,128)(2,1)S(1)}, bf16[128,512,128]{2,1,0:T(8,128)(2,1)}, bf16[128,512,128]{2,1,0:T(8,128)(2,1)}) custom-call(s32[128]{0:T(128)} %lens_ref.1, s32[1,128]{1,0:T(1,128)} %bitcast.18, f32[1,128]{1,0:T(1,128)} %constant.2.clone.freq_hbm, bf16[128,2048]{1,0:T(8,128)(2,1)} %refs_1_.1, bf16[2048]{0:T(1024)(128)(2,1)} %g_hbm.1, ...), custom_call_target="tpu_custom_call" | custom-call | tf_op jit(solution)/shard_map/attention/pallas_call | solution.py:521
  24.5 62.2 %tail.1 = (bf16[128,2048]{1,0:T(8,128)(2,1)S(1)}, f32[1,128]{1,0:T(1,128)S(1)}, f32[1,128]{1,0:T(1,128)S(1)}) custom-call(bf16[8,128,256]{2,1,0:T(8,128)(2,1)S(1)} %get-tuple-element.14.refs_0_, bf16[128,2048]{1,0:T(8,128)(2,1)} %refs_1_.1, bf16[2048]{0:T(1024)(128)(2,1)} %refs_2_.1, bf16[2048]{0:T(1024)(128)(2,1)} %refs_3_.1, s32[1,128]{1,0:T(1,128)} %bitcast.19, ...), custom_call_target="tpu_custom_call" | custom-call | tf_op jit(solution)/shard_map/tail/pallas_call | solution.py:550
  86.7 0.8 emit.1

commit v11 on v10

--- a/solution.py
+++ b/solution.py
@@ -370,9 +370,17 @@
     chip_sum(len(SUM2) - 1)
     issue(1, 3 * n_mlp)
 
+    last = len(SUM2) - 1
+    straight = remote(part_of(y_s.at[0], mine, SUM2[last]), part_of(y_s.at[1], mine, SUM2[last]), s_f.at[last], r_f.at[last], (1 - dp, tp + 1 - 2 * core))
+
     def forward(i):
         yy[i].wait_recv()
-        yf[i].start()
+        if i < last:
+            yf[i].start()
+        else:
+            @pl.when(core == 1)
+            def _():
+                yf[i].start()
 
     for i, (first, n) in enumerate(SUM2):
         x2[i].wait_recv()
@@ -381,6 +389,10 @@
             total = s2[j].astype(F32) + r2b[j].astype(F32)
             y_s[0, mine + j] = (a_s[mine + j].astype(F32) + total).astype(BF16)
         yy[i].start()
+        if i == last:
+            @pl.when(core == 0)
+            def _():
+                straight.start()
         yo[i].start()
     for i in range(len(SUM2)):
         forward(i)

time: 87.9 us -> 87.6 us (level)
  no operation moved by 1% of the time
where the time goes in v11:
time: 87.6 us; the launch traced here: 87.4 us
  Pallas kernels  86.6 us (99%)
    pallas_call x1, Pallas kernels, local_step(): pl.pallas_call(kernel, out_shape=(pltpu.VMEM((ROWS, WIDTH), BF16), pltpu....  61.9 us
    pallas_call x1, Pallas kernels, local_step(): pl.pallas_call(attn_kernel, out_shape=(pltpu.VMEM((NCH, ROWS, CHUNK), BF1...  23.9 us

profile of v11, /device:TPU:0, one launch (start us, length us, event | category | flops | bytes accessed | tf_op | source)
XLA Modules:
  0.0 87.4 jit_solution(13287675890766325575)
XLA Ops:
  0.6 23.9 %attention.1 = (bf16[8,128,256]{2,1,0:T(8,128)(2,1)S(1)}, bf16[128,512,128]{2,1,0:T(8,128)(2,1)}, bf16[128,512,128]{2,1,0:T(8,128)(2,1)}) custom-call(s32[128]{0:T(128)} %lens_ref.1, s32[1,128]{1,0:T(1,128)} %bitcast.18, f32[1,128]{1,0:T(1,128)} %constant.2.clone.freq_hbm, bf16[128,2048]{1,0:T(8,128)(2,1)} %refs_1_.1, bf16[2048]{0:T(1024)(128)(2,1)} %g_hbm.1, ...), custom_call_target="tpu_custom_call" | custom-call | tf_op jit(solution)/shard_map/attention/pallas_call | solution.py:533
  24.5 61.9 %tail.1 = (bf16[128,2048]{1,0:T(8,128)(2,1)S(1)}, f32[1,128]{1,0:T(1,128)S(1)}, f32[1,128]{1,0:T(1,128)S(1)}) custom-call(bf16[8,128,256]{2,1,0:T(8,128)(2,1)S(1)} %get-tuple-element.14.refs_0_, bf16[128,2048]{1,0:T(8,128)(2,1)} %refs_1_.1, bf16[2048]{0:T(1024)(128)(2,1)} %refs_2_.1, bf16[2048]{0:T(1024)(128)(2,1)} %refs_3_.1, s32[1,128]{1,0:T(1,128)} %bitcast.19, ...), custom_call_target="tpu_custom_call" | custom-call | tf_op jit(solution)/shard_map/tail/pallas_call | solution.py:562
  86.4 0.8 emit.1
